TPU v7x, 128 devices: a whole 4x4x4 slice. The times are simulated.
128 devices in a mesh: rows: 16 (over y, z), groups: 8 (over x, core).
Axes of the slice: x: 4, y: 4, z: 4, core: 2. Of those that a mesh axis runs over, the one named last changes fastest.
Arguments:
- basis: bfloat16 [8, 524288, 128], P(None, ('rows', 'groups')), may hold values from -6 to 6
- image: bfloat16 [8, 524288, 128], P(None, ('rows', 'groups')), may hold values from -6 to 6
- selection: int32 [8, 64], replicated, may hold values from 0 to 127, all different within a row
Outputs:
- rotated: bfloat16 [8, 524288, 128], P(None, ('rows', 'groups'))
Inputs may be any that keep to these rules, and one draw needn't show every extreme that they name: Each row of selection names 64 different columns.
All inputs are finite; a program needn't handle non-finite values.
Results may differ from a plain program's by a relative error of at most 0.005.
Values may be sent and summed in bfloat16 or wider, within the bound.
A program may use at most 128 MiB of HBM per device.

v0:
```python
import jax
import jax.numpy as jnp
from jax import lax
from jax.sharding import PartitionSpec as P

ITERS = 3


def in_blocks(shard, dim, devices):
    before, after = (shard.shape[:dim], shard.shape[dim + 1 :])
    return jnp.moveaxis(shard.reshape(*before, devices, -1, *after), dim, 0)


def sent_and_summed(shard, axis, dim):
    pieces = in_blocks(shard, dim, lax.axis_size(axis))
    arrived = lax.all_to_all(pieces, axis, split_axis=0, concat_axis=0, tiled=True)
    return arrived.sum(axis=0)


def from_everyone(shard, axis):
    copies = jnp.broadcast_to(shard, (lax.axis_size(axis), *shard.shape))
    return lax.all_to_all(copies, axis, split_axis=0, concat_axis=0, tiled=True)


def over_copies(shard, axis):
    return from_everyone(shard, axis).sum(axis=0)


def joined_along(pieces, dim):
    pieces = jnp.moveaxis(pieces, 0, dim)
    shape = pieces.shape
    return pieces.reshape(*shape[:dim], shape[dim] * shape[dim + 1], *shape[dim + 2 :])


def collect(shard, axis, dim):
    return joined_along(from_everyone(shard, axis), dim)


def small_solve(grams, chosen, total_rows):
    gram_s, cross, gram_f = (grams[0], grams[1], grams[2])
    width = gram_s.shape[0]
    coeffs = (jnp.arange(width, dtype=jnp.int32)[:, None] == chosen[None, :]).astype(jnp.float32)
    factor = jnp.linalg.cholesky(gram_f)
    for step in range(ITERS):
        moved = jnp.dot(cross.T, coeffs, precision=lax.Precision.HIGHEST)
        halfway = lax.linalg.triangular_solve(factor, moved, left_side=True, lower=True)
        solved = lax.linalg.triangular_solve(
            factor, halfway, left_side=True, lower=True, transpose_a=True
        )
        metric = (
            jnp.dot(
                solved.T,
                jnp.dot(gram_s, solved, precision=lax.Precision.HIGHEST),
                precision=lax.Precision.HIGHEST,
            )
            / total_rows
        )
        lower = jnp.linalg.cholesky(metric)
        coeffs = lax.linalg.triangular_solve(
            lower, solved, left_side=False, lower=True, transpose_a=True
        )
    return coeffs


def on_device(basis, image, selection):
    total_rows = basis.shape[1] * lax.axis_size("rows") * lax.axis_size("groups")
    gram_s = jnp.einsum("srk,srl->skl", basis, basis, preferred_element_type=jnp.float32)
    cross = jnp.einsum("srk,srl->skl", basis, image, preferred_element_type=jnp.float32)
    gram_f = jnp.einsum("srk,srl->skl", image, image, preferred_element_type=jnp.float32)
    partial_grams = jnp.stack([gram_s, cross, gram_f], axis=1)
    solver = jax.vmap(lambda grams, chosen: small_solve(grams, chosen, total_rows))
    shares = sent_and_summed(partial_grams, "groups", 0)
    summed = over_copies(shares, "rows")
    grams = summed
    count = shares.shape[0]
    start = lax.axis_index("groups") * count
    mine = lax.dynamic_slice_in_dim(selection, start, count, 0)
    local_coeffs = solver(grams, mine).astype(jnp.bfloat16)
    narrow = collect(local_coeffs, "groups", 0)
    first = jnp.einsum("srk,skj->srj", basis, narrow, preferred_element_type=jnp.float32)
    second = jnp.einsum("srk,skj->srj", image, narrow, preferred_element_type=jnp.float32)
    return jnp.concatenate([first, second], axis=2).astype(jnp.bfloat16)


def solution(mesh):
    in_specs = (P(None, ("rows", "groups"), None), P(None, ("rows", "groups"), None), P())
    out_specs = P(None, ("rows", "groups"), None)
    return jax.shard_map(
        on_device, mesh=mesh, in_specs=in_specs, out_specs=out_specs, check_vma=False
    )
```

profile of v0, /device:TPU:1, one launch (start us, length us, event | category | flops | bytes accessed | tf_op | source)
XLA Modules:
  0.0 205.5 jit_solution(12053994110823028597)
XLA Ops:
  0.0 8.4 %convolution_bitcast_fusion.2 = f32[8,1,128,128]{3,2,0,1:T(8,128)S(1)} fusion(bf16[8,4096,128]{2,1,0:T(8,128)(2,1)} %param.10), kind=kOutput, calls=%fused_computation.8 | convolution fusion | flops 1073741824 | bytes 8912896 | tf_op jit(solution)/shard_map/srk,srl->skl/dot_general | solution.py:67
  8.4 5.9 %convolution_bitcast_fusion.1 = f32[8,1,128,128]{3,2,0,1:T(8,128)S(1)} fusion(bf16[8,4096,128]{2,1,0:T(8,128)(2,1)} %param.10, bf16[8,4096,128]{2,1,0:T(8,128)(2,1)S(1)} %copy-done.1), kind=kOutput, calls=%fused_computation.7 | convolution fusion | flops 1073741824 | bytes 17301504 | tf_op jit(solution)/shard_map/srk,srl->skl/dot_general | solution.py:68
  14.3 2.5 %convolution_bitcast_fusion = f32[8,1,128,128]{3,2,0,1:T(8,128)S(1)} fusion(bf16[8,4096,128]{2,1,0:T(8,128)(2,1)S(1)} %copy-done.1), kind=kOutput, calls=%fused_computation.6 | convolution fusion | flops 1073741824 | bytes 8912896 | tf_op jit(solution)/shard_map/srk,srl->skl/dot_general | solution.py:69
  17.1 26.1 %all_to_all.15 = f32[8,1,3,128,128]{4,3,2,1,0:T(8,128)S(1)} all-to-all(f32[8,1,3,128,128]{4,3,2,1,0:T(8,128)S(1)} %copy.41), channel_id=1, replica_groups=mesh['rows'=16,'groups'=8] {'groups'}, dimensions={0} | all-to-all | bytes 3145728 | tf_op jit(solution)/shard_map/all_to_all | solution.py:16
  43.3 2.0 broadcast_in_dim.8
  45.4 7.9 %all-to-all-start.1 = ((f32[16,1,3,128,128]{4,3,2,1,0:T(8,128)}), f32[16,1,3,128,128]{4,3,2,1,0:T(8,128)S(1)}, u32[]{:S(2)}, u32[]{:S(2)}) async-start(f32[16,1,3,128,128]{4,3,2,1,0:T(8,128)} %broadcast_in_dim.8), calls=%async_computation.1 | async-start | bytes 6291456 | tf_op jit(solution)/shard_map/all_to_all | solution.py:22
  53.3 40.3 %all-to-all-done.1 = f32[16,1,3,128,128]{4,3,2,1,0:T(8,128)S(1)} async-done(((f32[16,1,3,128,128]{4,3,2,1,0:T(8,128)}), f32[16,1,3,128,128]{4,3,2,1,0:T(8,128)S(1)}, u32[]{:S(2)}, u32[]{:S(2)}) %all-to-all-start.1) | async-done | bytes 3145760 | tf_op jit(solution)/shard_map/all_to_all | solution.py:22
  94.3 11.7 %custom-call.16 = f32[1,128,128]{2,1,0:T(8,128)S(1)} custom-call(f32[1,128,128]{2,1,0:T(8,128)S(1)} %fusion.7), custom_call_target="Cholesky" | custom-call | tf_op jit(solution)/shard_map/vmap(jit(cholesky))/cholesky | solution.py:43
  106.1 0.6 compare_reduce_fusion.3
  106.7 0.7 fusion.6
  107.4 9.8 %custom-call.34 = f32[1,1,128,128]{2,3,1,0:T(8,128)S(1)} custom-call(f32[1,1,128,128]{3,2,1,0:T(8,128)S(1)} %fusion.6), custom_call_target="InvertDiagBlocksLowerTriangular" | custom-call | tf_op jit(solution)/shard_map/vmap()/triangular_solve/custom-call.3 | solution.py:47
  118.1 5.8 %custom-call.27 = f32[1,64,64]{2,1,0:T(8,128)S(1)} custom-call(f32[1,64,64]{2,1,0:T(8,128)S(1)} %fusion.31), custom_call_target="Cholesky" | custom-call | tf_op jit(solution)/shard_map/vmap(jit(cholesky))/cholesky | solution.py:58
  124.0 0.6 compare_reduce_fusion.2
  124.6 0.7 fusion.26
  125.3 4.9 %custom-call.28 = f32[1,1,64,64]{2,3,1,0:T(8,128)S(1)} custom-call(f32[1,1,64,64]{3,2,1,0:T(8,128)S(1)} %fusion.26), custom_call_target="InvertDiagBlocksLowerTriangular" | custom-call | tf_op jit(solution)/shard_map/vmap()/triangular_solve/custom-call.4 | solution.py:59
  130.2 0.3 convolution_bitcast_fusion.5
  130.4 0.2 fusion.21
  131.6 5.8 %custom-call.31 = f32[1,64,64]{2,1,0:T(8,128)S(1)} custom-call(f32[1,64,64]{2,1,0:T(8,128)S(1)} %fusion.30), custom_call_target="Cholesky" | custom-call | tf_op jit(solution)/shard_map/vmap(jit(cholesky))/cholesky | solution.py:58
  137.5 0.6 compare_reduce_fusion.1
  138.1 0.7 fusion.27
  138.8 4.9 %custom-call.32 = f32[1,1,64,64]{2,3,1,0:T(8,128)S(1)} custom-call(f32[1,1,64,64]{3,2,1,0:T(8,128)S(1)} %fusion.27), custom_call_target="InvertDiagBlocksLowerTriangular" | custom-call | tf_op jit(solution)/shard_map/vmap()/triangular_solve/custom-call.4 | solution.py:59
  143.7 0.3 convolution_bitcast_fusion.4
  145.1 6.0 %custom-call.35 = f32[1,64,64]{2,1,0:T(8,128)S(1)} custom-call(f32[1,64,64]{2,1,0:T(8,128)S(1)} %fusion.29), custom_call_target="Cholesky" | custom-call | tf_op jit(solution)/shard_map/vmap(jit(cholesky))/cholesky | solution.py:58
  151.2 0.6 compare_reduce_fusion
  151.8 0.7 fusion.28
  152.5 4.9 %custom-call.36 = f32[1,1,64,64]{2,3,1,0:T(8,128)S(1)} custom-call(f32[1,1,64,64]{3,2,1,0:T(8,128)S(1)} %fusion.28), custom_call_target="InvertDiagBlocksLowerTriangular" | custom-call | tf_op jit(solution)/shard_map/vmap()/triangular_solve/custom-call.4 | solution.py:59
  157.4 0.3 fusion.3
  157.7 11.3 %all_to_all.16 = bf16[8,1,128,64]{2,3,1,0:T(8,128)(2,1)S(1)} all-to-all(bf16[8,1,128,64]{2,3,1,0:T(8,128)(2,1)S(1)} %broadcast_in_dim.11), channel_id=1, replica_groups=mesh['rows'=16,'groups'=8] {'groups'}, dimensions={0} | all-to-all | bytes 262144 | tf_op jit(solution)/shard_map/all_to_all | solution.py:22
  169.0 8.4 %fusion.1 = bf16[8,4096,64]{1,2,0:T(8,128)(2,1)} fusion(bf16[8,4096,128]{2,1,0:T(8,128)(2,1)} %param.11, bf16[8,1,128,64]{2,3,1,0:T(8,128)(2,1)S(1)} %all_to_all.16), kind=kOutput, calls=%fused_computation.4 | convolution fusion | flops 538968064 | bytes 12713984 | tf_op jit(solution)/shard_map/srk,skj->srj/dot_general | solution.py:81
  177.4 8.4 %fusion = bf16[8,4096,64]{1,2,0:T(8,128)(2,1)} fusion(bf16[8,4096,128]{2,1,0:T(8,128)(2,1)} %param.10, bf16[8,1,128,64]{2,3,1,0:T(8,128)(2,1)S(1)} %all_to_all.16), kind=kOutput, calls=%fused_computation.3 | convolution fusion | flops 538968064 | bytes 12713984 | tf_op jit(solution)/shard_map/srk,skj->srj/dot_general | solution.py:80
  185.8 7.8 %pad_maximum_fusion = bf16[8,4096,128]{1,2,0:T(8,128)(2,1)} fusion(bf16[8,4096,64]{1,2,0:T(8,128)(2,1)} %fusion.1, bf16[8,4096,64]{1,2,0:T(8,128)(2,1)} %fusion), kind=kLoop, calls=%fused_computation | loop fusion | flops 16777216 | bytes 16777216 | tf_op jit(solution)/shard_map/concatenate | solution.py:82
  193.6 11.9 %copy.50 = bf16[8,4096,128]{2,1,0:T(8,128)(2,1)} copy(bf16[8,4096,128]{1,2,0:T(8,128)(2,1)} %pad_maximum_fusion) | data formatting | bytes 16777216 | tf_op jit(solution)/shard_map/concatenate | solution.py:82
  (38 shorter events, 4.0 us)
Async XLA Ops:
  0.0 53.3 %copy-start = (s32[8,64]{1,0:T(8,128)S(1)}, s32[8,64]{1,0:T(8,128)}, u32[]{:S(2)}) copy-start(s32[8,64]{1,0:T(8,128)} %param.12) | copy-start | bytes 6148
  0.0 8.4 %copy-start.1 = (bf16[8,4096,128]{2,1,0:T(8,128)(2,1)S(1)}, bf16[8,4096,128]{2,1,0:T(8,128)(2,1)}, u32[]{:S(2)}) copy-start(bf16[8,4096,128]{2,1,0:T(8,128)(2,1)} %param.11) | copy-start | bytes 25165828
  45.4 48.3 %all-to-all-start.1 = ((f32[16,1,3,128,128]{4,3,2,1,0:T(8,128)}), f32[16,1,3,128,128]{4,3,2,1,0:T(8,128)S(1)}, u32[]{:S(2)}, u32[]{:S(2)}) async-start(f32[16,1,3,128,128]{4,3,2,1,0:T(8,128)} %broadcast_in_dim.8), calls=%async_computation.1 | async-start | bytes 6291456 | tf_op jit(solution)/shard_map/all_to_all | solution.py:22
where the time goes:
time: 206 us
  other arithmetic  67.5 us (33%)
  waiting for transfers between devices  40.3 us (20%)
  blocking collectives  37.5 us (18%)
  matrix products  37.4 us (18%)
  local copies, waits for them, and re-layouts  14.6 us (7%)
  starting transfers between devices  7.95 us (4%)
    all_to_all x1, waiting for transfers between devices, from_everyone(): return lax.all_to_all(copies, axis, split_axis=0, concat_axis=0, tiled=True)  40.3 us
    all_to_all x1, blocking collectives, sent_and_summed(): lax.all_to_all(pieces, axis, split_axis=0, concat_axis=0, tiled=True)  26.1 us
    another operation x9, other arithmetic, small_solve(): lower = jnp.linalg.cholesky(metric)  19.8 us
    another operation x6, other arithmetic, small_solve(): lax.linalg.triangular_solve(lower, solved, left_side=False, lower=True, t...  16.6 us
    another operation x3, other arithmetic, small_solve(): factor = jnp.linalg.cholesky(gram_f)  12.4 us
    concatenate x1, local copies, waits for them, and re-layouts, on_device(): return jnp.concatenate([first, second], axis=2).astype(jnp.bfloat16)  11.9 us
    all_to_all x1, blocking collectives, from_everyone(): return lax.all_to_all(copies, axis, split_axis=0, concat_axis=0, tiled=True)  11.3 us
    another operation x2, other arithmetic, small_solve(): lax.linalg.triangular_solve(factor, halfway, left_side=True, lower=True,...  10.5 us
  transfers between devices with their start and end apart: 1, of which 1 were waited for; matrix products, arithmetic and copies ran while one was open for 0% of the time, Pallas kernels for 0%

commit v1 on v0

v1 whole, which is shorter than its diff:
```python
import functools

import jax
import jax.numpy as jnp
from jax import lax
from jax.experimental import pallas as pl
from jax.experimental.pallas import tpu as pltpu
from jax.sharding import PartitionSpec as P

ITERS = 3
F32 = jnp.float32
BF16 = jnp.bfloat16
HIGHEST = lax.Precision.HIGHEST
SYSTEMS = 8
DEPTH = 4096
COLS = 128
KEPT = 64
CHIPS = 64
PLANE = 16


def dot(a, b, over_a, over_b):
    dims = (((over_a,), (over_b,)), ((), ()))
    return lax.dot_general(a, b, dims, precision=HIGHEST, preferred_element_type=F32)


def lane(tile, j):
    return jnp.broadcast_to(tile[:, j : j + 1], (8, 128))


def row(tile, j):
    return jnp.broadcast_to(tile[j : j + 1, :], (8, 128))


def added(parts):
    while len(parts) > 1:
        parts = [parts[i] + parts[i + 1] for i in range(0, len(parts), 2)]
    return parts[0]


def times(cols, tile):
    return added([cols[j] * row(tile, j) for j in range(8)])


def less(tile, cols, rows):
    return tile - added([cols[j] * rows[j] for j in range(8)])


def pivot(v, j, at, r):
    piv = v[j]
    for other in range(8):
        if other != j:
            w = row(v[other], j) * r
            v[other] = jnp.where(at, w, v[other] - piv * w)
    v[j] = jnp.where(at, r, -(piv * r))


def solved_rows(f, x, sub):
    n = len(f)
    for k in range(n):
        cols = [[lane(f[i], 8 * k + j) for j in range(8)] for i in range(n)]
        v = list(cols[k])
        for j in range(8):
            pivot(v, j, sub == j, 1.0 / row(v[j], j))
        fk, xk = times(v, f[k]), times(v, x[k])
        fr = [row(fk, j) for j in range(8)]
        xr = [row(xk, j) for j in range(8)]
        for i in list(range(k + 1, n)) + list(range(k)):
            if k < n - 1:
                f[i] = less(f[i], cols[i], fr)
            x[i] = less(x[i], cols[i], xr)
        f[k], x[k] = fk, xk
    return x


def normalised_rows(m, y, sub):
    n = len(m)
    out = []
    for k in range(n):
        cols = [[lane(m[i], 8 * k + j) for j in range(8)] for i in range(k, n)]
        v = list(cols[0])
        mine = y[k]
        scale = jnp.zeros((8, 128), F32)
        for j in range(8):
            p = row(v[j], j)
            r = 1.0 / p
            at = sub == j
            scale = jnp.where(at, p, scale)
            mine = mine - jnp.where(sub > j, v[j] * r, 0.0) * row(mine, j)
            pivot(v, j, at, r)
        out.append(mine * lax.rsqrt(scale))
        if k < n - 1:
            mk, yk = times(v, m[k]), times(v, y[k])
            mr = [row(mk, j) for j in range(8)]
            yr = [row(yk, j) for j in range(8)]
            for i in range(k + 1, n):
                m[i] = less(m[i], cols[i - k], mr)
                y[i] = less(y[i], cols[i - k], yr)
    return out


def tiles(a):
    return [a[8 * i : 8 * i + 8] for i in range(a.shape[0] // 8)]


def gather_kernel(
    total_rows, w_hbm, q_hbm, chosen_ref, out_ref,
    wq, lent, given, sums, arrived, pieces, coeffs, local_coeffs,
    load_sem, lent_sem, given_sem, send_sem, recv_sem,
    share_send, share_recv, done_send, done_recv,
):
    me_row, me_group = lax.axis_index("rows"), lax.axis_index("groups")
    x, core = me_group // 2, lax.rem(me_group, 2)
    y, z = me_row // 4, lax.rem(me_row, 4)

    def system(step):
        hop = (2, 1, 3, 0)[step // 2]
        parity = 1 - core if step % 2 == 0 else core
        return 2 * lax.rem(x + hop, 4) + parity

    def load(step):
        s = system(step)
        return [
            pltpu.make_async_copy(ref.at[s], wq.at[step, :, pl.ds(off, COLS)], load_sem.at[step, i])
            for i, (ref, off) in enumerate(((w_hbm, 0), (q_hbm, COLS)))
        ]

    ahead = 4
    for step in range(ahead):
        for copy in load(step):
            copy.start()

    barrier = pltpu.get_barrier_semaphore()

    def at_chip(i):
        dx, dy, dz = i // 16, lax.rem(i // 4, 4), lax.rem(i, 4)
        rows = lax.rem(y + dy, 4) * 4 + lax.rem(z + dz, 4)
        return rows, lax.rem(x + dx, 4)

    def greet(i, _):
        rows, chip_x = at_chip(i)
        pl.semaphore_signal(
            barrier, inc=1, device_id={"rows": rows, "groups": 2 * chip_x + core},
            device_id_type=pl.DeviceIdType.MESH,
        )
        return 0

    lax.fori_loop(1, CHIPS, greet, 0)
    for hop in range(4):
        pl.semaphore_signal(
            barrier, inc=1,
            device_id={"rows": me_row, "groups": 2 * lax.rem(x + hop, 4) + 1 - core},
            device_id_type=pl.DeviceIdType.MESH,
        )

    def gram(step, ref):
        for copy in load(step):
            copy.wait()
        block = wq[step]
        g = lax.dot_general(block, block, (((0,), (0,)), ((), ())), preferred_element_type=F32)
        ref[:, 0:8, :] = g[:COLS, :COLS].reshape(PLANE, 8, COLS)
        ref[:, 8:16, :] = g[COLS:, :COLS].reshape(PLANE, 8, COLS)
        ref[:, 16:24, :] = g[COLS:, COLS:].reshape(PLANE, 8, COLS)
        if step + ahead < 8:
            for copy in load(step + ahead):
                copy.start()

    def lend(k):
        return pltpu.make_async_remote_copy(
            src_ref=lent.at[k], dst_ref=given.at[k], send_sem=lent_sem.at[k], recv_sem=given_sem.at[k],
            device_id={"rows": me_row, "groups": 2 * x + 1 - core}, device_id_type=pl.DeviceIdType.MESH,
        )

    def scatter(k):
        hop = (2, 1, 3, 0)[k]

        def send(j, _):
            rows, chip_x = at_chip(16 * hop + j)
            pltpu.make_async_remote_copy(
                src_ref=sums.at[k, rows], dst_ref=arrived.at[16 * hop + j],
                send_sem=send_sem, recv_sem=recv_sem,
                device_id={"rows": rows, "groups": 2 * chip_x + core}, device_id_type=pl.DeviceIdType.MESH,
            ).start()
            return 0

        if hop == 0:
            arrived[0] = sums[k, me_row]
        lax.fori_loop(1 if hop == 0 else 0, PLANE, send, 0)

    gram(0, lent.at[0])
    pl.semaphore_wait(barrier, CHIPS - 1 + 4)
    lend(0).start()
    for k in range(4):
        gram(2 * k + 1, sums.at[k])
        if k < 3:
            gram(2 * k + 2, lent.at[k + 1])
            lend(k + 1).start()
        lend(k).wait_recv()
        sums[k] = sums[k] + given[k]
        scatter(k)

    others = arrived.at[pl.ds(1, CHIPS - 1)]
    pltpu.make_async_copy(others, others, recv_sem).wait()

    def add(i, total):
        return tuple(t + arrived[i, 8 * n : 8 * n + 8, :] for n, t in enumerate(total))

    total = lax.fori_loop(
        1, CHIPS, add, tuple(arrived[0, 8 * n : 8 * n + 8, :] for n in range(3)), unroll=7
    )
    for n in range(3):
        pieces[me_row, 8 * n : 8 * n + 8, :] = total[n]

    def share(j, _):
        rows, _chip = at_chip(j)
        pltpu.make_async_remote_copy(
            src_ref=pieces.at[me_row], dst_ref=pieces.at[me_row], send_sem=share_send, recv_sem=share_recv,
            device_id={"rows": rows, "groups": me_group}, device_id_type=pl.DeviceIdType.MESH,
        ).start()
        return 0

    lax.fori_loop(1, PLANE, share, 0)
    fifteen = pieces.at[pl.ds(0, PLANE - 1)]
    pltpu.make_async_copy(fifteen, fifteen, share_recv).wait()

    sub = lax.broadcasted_iota(jnp.int32, (8, 128), 0)
    chosen = chosen_ref[pl.ds(me_group, 1), :]
    first = (lax.broadcasted_iota(jnp.int32, (COLS, KEPT), 0) == chosen).astype(F32).T
    gram_s = jnp.concatenate([pieces[i, 0:8, :] for i in range(PLANE)], axis=0)
    step_matrix = jnp.concatenate(
        solved_rows(
            [pieces[i, 16:24, :] for i in range(PLANE)], [pieces[i, 8:16, :] for i in range(PLANE)], sub
        ),
        axis=0,
    )
    metric_step = dot(gram_s, step_matrix, 1, 0)
    coeffs[...] = first

    def iterate(i, _):
        now = coeffs[...]
        moved = dot(now, step_matrix, 1, 1)
        metric = dot(moved, dot(now, metric_step, 1, 1), 1, 1) * (1.0 / total_rows)
        wide = jnp.concatenate([metric, jnp.zeros((KEPT, COLS - KEPT), F32)], axis=1)
        coeffs[...] = jnp.concatenate(normalised_rows(tiles(wide), tiles(moved), sub), axis=0)
        return 0

    lax.fori_loop(0, ITERS, iterate, 0)
    local_coeffs[...] = coeffs[...].astype(BF16)
    out_ref[me_group] = local_coeffs[...]

    def tell(i, _):
        pltpu.make_async_remote_copy(
            src_ref=local_coeffs, dst_ref=out_ref.at[me_group], send_sem=done_send, recv_sem=done_recv,
            device_id={"rows": me_row, "groups": lax.rem(me_group + i, SYSTEMS)},
            device_id_type=pl.DeviceIdType.MESH,
        ).start()
        return 0

    lax.fori_loop(1, SYSTEMS, tell, 0)
    seven = out_ref.at[pl.ds(0, SYSTEMS - 1)]
    pltpu.make_async_copy(seven, seven, done_recv).wait()
    pltpu.make_async_copy(seven, seven, done_send).wait()
    pltpu.make_async_copy(fifteen, fifteen, share_send).wait()
    pltpu.make_async_copy(others, others, send_sem).wait()
    for k in range(4):
        lend(k).wait_send()


def gathered(basis, image, selection, total_rows):
    piece = (24, COLS)
    dma = pltpu.SemaphoreType.DMA
    return pl.pallas_call(
        functools.partial(gather_kernel, total_rows),
        out_shape=jax.ShapeDtypeStruct((SYSTEMS, KEPT, COLS), BF16),
        in_specs=[
            pl.BlockSpec(memory_space=pltpu.HBM),
            pl.BlockSpec(memory_space=pltpu.HBM),
            pl.BlockSpec(memory_space=pltpu.VMEM),
        ],
        out_specs=pl.BlockSpec(memory_space=pltpu.VMEM),
        scratch_shapes=[
            pltpu.VMEM((SYSTEMS, DEPTH, 2 * COLS), BF16),
            pltpu.VMEM((4, PLANE, *piece), F32),
            pltpu.VMEM((4, PLANE, *piece), F32),
            pltpu.VMEM((4, PLANE, *piece), F32),
            pltpu.VMEM((CHIPS, *piece), F32),
            pltpu.VMEM((PLANE, *piece), F32),
            pltpu.VMEM((KEPT, COLS), F32),
            pltpu.VMEM((KEPT, COLS), BF16),
            dma((SYSTEMS, 2)),
            dma((4,)),
            dma((4,)),
            dma, dma, dma, dma, dma, dma,
        ],
        compiler_params=pltpu.CompilerParams(
            collective_id=0, has_side_effects=True, vmem_limit_bytes=40 * 2**20
        ),
        name="gather_solve",
    )(basis, image, selection)


def rotate_kernel(w_ref, q_ref, c_ref, o_ref, both):
    @pl.when(pl.program_id(1) == 0)
    def _():
        both[...] = jnp.zeros_like(both)
        both[:KEPT, :COLS] = c_ref[0]
        both[KEPT:, COLS:] = c_ref[0]

    rows = jnp.concatenate([w_ref[0], q_ref[0]], axis=1)
    o_ref[0] = lax.dot_general(
        rows, both[...], (((1,), (1,)), ((), ())), preferred_element_type=F32
    ).astype(BF16)


def rotated(basis, image, coeffs):
    block = 2048
    data = pl.BlockSpec((1, block, COLS), lambda s, i: (s, i, 0))
    return pl.pallas_call(
        rotate_kernel,
        grid=(SYSTEMS, DEPTH // block),
        out_shape=jax.ShapeDtypeStruct((SYSTEMS, DEPTH, COLS), BF16),
        in_specs=[data, data, pl.BlockSpec((1, KEPT, COLS), lambda s, i: (s, 0, 0))],
        out_specs=data,
        scratch_shapes=[pltpu.VMEM((2 * KEPT, 2 * COLS), BF16)],
        name="rotate",
    )(basis, image, coeffs)


def on_device(basis, image, selection):
    total_rows = basis.shape[1] * lax.axis_size("rows") * lax.axis_size("groups")
    coeffs = gathered(basis, image, selection, total_rows)
    return rotated(basis, image, coeffs)


def solution(mesh):
    in_specs = (P(None, ("rows", "groups"), None), P(None, ("rows", "groups"), None), P())
    out_specs = P(None, ("rows", "groups"), None)
    return jax.shard_map(
        on_device, mesh=mesh, in_specs=in_specs, out_specs=out_specs, check_vma=False
    )
```

time: 206 us -> 78.1 us (0.38)
  Pallas kernels: 0 us -> 72.8 us
  other arithmetic: 67.5 us -> 0 us
  waiting for transfers between devices: 40.3 us -> 0 us
  blocking collectives: 37.5 us -> 0 us
  matrix products: 37.4 us -> 0 us
  local copies, waits for them, and re-layouts: 14.6 us -> 4.71 us
  starting transfers between devices: 7.95 us -> 0 us
    pallas_call x0 -> x2, Pallas kernels: none -> 72.8 us  [the longest x1 56.4 us: gathered(): pl.pallas_call(functools.partial(gather_kernel, total_rows), out_shape=ja...]
    another operation x20 -> x0, other arithmetic: 59.3 us -> none  [the longest x9 19.8 us: small_solve(): lower = jnp.linalg.cholesky(metric)]
    all_to_all x1 -> x0, waiting for transfers between devices: 40.3 us -> none  [from_everyone(): return lax.all_to_all(copies, axis, split_axis=0, concat_axis=0, tiled=True)]
    all_to_all x2 -> x0, blocking collectives: 37.5 us -> none  [the longest x1 26.1 us: sent_and_summed(): lax.all_to_all(pieces, axis, split_axis=0, concat_axis=0, tiled=True)]
    dot_general x14 -> x0, matrix products: 35.4 us -> none  [the longest x1 8.41 us: on_device(): jnp.einsum('srk,skj->srj', image, narrow, preferred_element_type=jnp.floa...]
    concatenate x1 -> x0, local copies, waits for them, and re-layouts: 11.9 us -> none  [on_device(): return jnp.concatenate([first, second], axis=2).astype(jnp.bfloat16)]
    all_to_all x1 -> x0, starting transfers between devices: 7.95 us -> none  [from_everyone(): return lax.all_to_all(copies, axis, split_axis=0, concat_axis=0, tiled=True)]
    concatenate x1 -> x0, other arithmetic: 7.8 us -> none  [on_device(): return jnp.concatenate([first, second], axis=2).astype(jnp.bfloat16)]
  transfers between devices with their start and end apart: 1 -> 0, of which waited for: 1 -> 0; matrix products, arithmetic and copies ran while one was open for 0% -> 0% of each run, Pallas kernels for 0% -> 0%
where the time goes in v1:
time: 78.1 us; the launch traced here: 77.6 us
  Pallas kernels  72.8 us (93%)
  local copies, waits for them, and re-layouts  4.71 us (6%)
    pallas_call x1, Pallas kernels, gathered(): pl.pallas_call(functools.partial(gather_kernel, total_rows), out_shape=ja...  56.4 us
    pallas_call x1, Pallas kernels, rotated(): pl.pallas_call(rotate_kernel, grid=(SYSTEMS, DEPTH // block), out_shape=j...  16.4 us
    unnamed x6, local copies, waits for them, and re-layouts  4.71 us

profile of v1, /device:TPU:1, one launch (start us, length us, event | category | flops | bytes accessed | tf_op | source)
XLA Modules:
  0.0 77.6 jit_solution(3736645016711749623)
XLA Ops:
  0.0 0.0 copy-start
  0.0 3.4 %copy-done = bf16[8,4096,128]{2,1,0:T(8,128)(2,1)S(1)} copy-done((bf16[8,4096,128]{2,1,0:T(8,128)(2,1)S(1)}, bf16[8,4096,128]{2,1,0:T(8,128)(2,1)}, u32[]{:S(2)}) %copy-start) | copy-done | bytes 8388632
  3.4 0.0 copy-start.2
  3.4 0.7 copy-done.2
  4.1 56.4 %gather_solve.1.c_ref = bf16[8,64,128]{2,1,0:T(8,128)(2,1)S(1)} custom-call(bf16[8,4096,128]{2,1,0:T(8,128)(2,1)S(1)} %copy-done, bf16[8,4096,128]{2,1,0:T(8,128)(2,1)} %q_ref.1, s32[8,64]{1,0:T(8,128)S(1)} %copy-done.2), custom_call_target="tpu_custom_call" | custom-call | tf_op jit(solution)/shard_map/gather_solve/pallas_call | solution.py:272
  60.5 0.0 copy-start.1
  60.5 0.6 copy-done.1
  61.1 16.4 %rotate.1 = bf16[8,4096,128]{2,1,0:T(8,128)(2,1)} custom-call(bf16[8,4096,128]{2,1,0:T(8,128)(2,1)} %w_ref.1, bf16[8,4096,128]{2,1,0:T(8,128)(2,1)} %q_ref.1, bf16[8,64,128]{2,1,0:T(8,128)(2,1)} %copy-done.1), custom_call_target="tpu_custom_call" | custom-call | tf_op jit(solution)/shard_map/rotate/pallas_call | solution.py:318
Async XLA Ops:
  0.0 3.4 %copy-start = (bf16[8,4096,128]{2,1,0:T(8,128)(2,1)S(1)}, bf16[8,4096,128]{2,1,0:T(8,128)(2,1)}, u32[]{:S(2)}) copy-start(bf16[8,4096,128]{2,1,0:T(8,128)(2,1)} %w_ref.1) | copy-start | bytes 25165828
  3.4 0.7 copy-start.2
  60.5 0.6 copy-start.1

commit v2 on v1

v2 whole, which is shorter than its diff:
```python
import functools

import jax
import jax.numpy as jnp
from jax import lax
from jax.experimental import pallas as pl
from jax.experimental.pallas import tpu as pltpu
from jax.sharding import PartitionSpec as P

ITERS = 3
F32 = jnp.float32
BF16 = jnp.bfloat16
SYSTEMS = 8
DEPTH = 4096
COLS = 128
KEPT = 64
CHIPS = 64
PLANE = 16


def split(a):
    high = a.astype(BF16)
    rest = a - high.astype(F32)
    middle = rest.astype(BF16)
    return high, middle, (rest - middle.astype(F32)).astype(BF16)


def dot(a, b, over_a, over_b):
    dims = (((over_a,), (over_b,)), ((), ()))

    def both(p, q, r, s):
        return lax.dot_general(
            jnp.concatenate([p, q], axis=over_a), jnp.concatenate([r, s], axis=over_b), dims,
            preferred_element_type=F32,
        )

    (a1, a2, a3), (b1, b2, b3) = split(a), split(b)
    return both(a1, a2, b1, b1) + (both(a1, a2, b2, b2) + both(a1, a3, b3, b1))


def lane(tile, j):
    return jnp.broadcast_to(tile[:, j : j + 1], (8, 128))


def row(tile, j):
    return jnp.broadcast_to(tile[j : j + 1, :], (8, 128))


def added(parts):
    while len(parts) > 1:
        parts = [parts[i] + parts[i + 1] for i in range(0, len(parts), 2)]
    return parts[0]


def times(cols, tile):
    return added([cols[j] * row(tile, j) for j in range(8)])


def less(tile, cols, rows):
    return tile - added([cols[j] * rows[j] for j in range(8)])


def pivot(v, j, at, r):
    piv = v[j]
    for other in range(8):
        if other != j:
            w = row(v[other], j) * r
            v[other] = jnp.where(at, w, v[other] - piv * w)
    v[j] = jnp.where(at, r, -(piv * r))


def stacked(parts):
    return jnp.concatenate(parts, axis=0)


def tiles(a):
    return [a[8 * i : 8 * i + 8] for i in range(a.shape[0] // 8)]


def gauss_jordan(f, x, start, sub):
    for k in range(8):
        v = [lane(f[k], start + 8 * k + j) + 0.0 for j in range(8)]
        cols = {
            i: [lane(f[i], start + 8 * k + j) for j in range(8)]
            for i in [*range(k + 1, 8), *range(k)]
        }
        for j in range(8):
            pivot(v, j, sub == j, 1.0 / row(v[j], j))
        fk, xk = times(v, f[k]), times(v, x[k])
        fr = [row(fk, j) for j in range(8)]
        xr = [row(xk, j) for j in range(8)]
        for i in cols:
            f[i] = less(f[i], cols[i], fr)
            x[i] = less(x[i], cols[i], xr)
        f[k], x[k] = fk, xk


def solved(f, x, sub):
    half = f.shape[0] // 2
    left = lax.broadcasted_iota(jnp.int32, (half, 128), 1) < half
    zero = jnp.zeros((half, 128), F32)
    low = f[half:]
    ft, xt = tiles(f[:half]), tiles(x[:half])
    gauss_jordan(ft, xt, 0, sub)
    ft, xt = stacked(ft), stacked(xt)
    right = jnp.concatenate([stacked([ft, zero]), stacked([xt, zero])], axis=1)
    step = dot(jnp.where(left, low, 0.0), right, 1, 0)
    fl, xl = tiles(low - step[:, :128]), tiles(x[half:] - step[:, 128:])
    gauss_jordan(fl, xl, half, sub)
    xl = stacked(xl)
    return stacked([xt - dot(jnp.where(left, 0.0, ft), stacked([zero, xl]), 1, 0), xl])


def normalised_rows(m, y, sub):
    n = len(m)
    out = []
    for k in range(n):
        v = [lane(m[k], 8 * k + j) + 0.0 for j in range(8)]
        cols = {i: [lane(m[i], 8 * k + j) for j in range(8)] for i in range(k + 1, n)}
        mine = y[k]
        scale = jnp.zeros((8, 128), F32)
        for j in range(8):
            p = row(v[j], j)
            r = 1.0 / p
            at = sub == j
            scale = jnp.where(at, p, scale)
            mine = mine - jnp.where(sub > j, v[j] * r, 0.0) * row(mine, j)
            pivot(v, j, at, r)
        out.append(mine * lax.rsqrt(scale))
        if k < n - 1:
            mk, yk = times(v, m[k]), times(v, y[k])
            mr = [row(mk, j) for j in range(8)]
            yr = [row(yk, j) for j in range(8)]
            for i in cols:
                m[i] = less(m[i], cols[i], mr)
                y[i] = less(y[i], cols[i], yr)
    return out


def system_at(step, x, core):
    hop = (2, 1, 3, 0)[step // 2]
    return 2 * lax.rem(x + hop, 4) + (1 - core if step % 2 == 0 else core)


def gather_kernel(
    total_rows, w_hbm, q_hbm, chosen_hbm, out_ref, wq,
    chosen_ref, lent, given, sums, arrived, diagonals, pieces, coeffs, local_coeffs,
    load_sem, lent_sem, given_sem, send_sem, recv_sem, diag_send, diag_recv,
    share_send, share_recv, share_diag_send, share_diag_recv, done_send, done_recv, chosen_sem,
):
    me_row, me_group = lax.axis_index("rows"), lax.axis_index("groups")
    x, core = me_group // 2, lax.rem(me_group, 2)
    y, z = me_row // 4, lax.rem(me_row, 4)
    xs, ys, zs = ([lax.rem(c + d, 4) for d in range(4)] for c in (x, y, z))
    row_at = [4 * ys[j // 4] + zs[j % 4] for j in range(PLANE)]
    to_first = 4 * lax.rem(4 - y, 4) + lax.rem(4 - z, 4)

    def device(rows, groups):
        return dict(
            device_id={"rows": rows, "groups": groups}, device_id_type=pl.DeviceIdType.MESH
        )

    def landed(ref, sem):
        pltpu.make_async_copy(ref, ref, sem).wait()

    def load(step):
        s = system_at(step, x, core)
        return [
            pltpu.make_async_copy(ref.at[s], wq.at[step, :, pl.ds(off, COLS)], load_sem.at[step, i])
            for i, (ref, off) in enumerate(((w_hbm, 0), (q_hbm, COLS)))
        ]

    ahead = 4
    for step in range(ahead):
        for copy in load(step):
            copy.start()
    fetch_chosen = pltpu.make_async_copy(chosen_hbm, chosen_ref, chosen_sem)
    fetch_chosen.start()

    barrier = pltpu.get_barrier_semaphore()
    for hop in range(4):
        pl.semaphore_signal(barrier, inc=1, **device(me_row, 2 * xs[hop] + 1 - core))
        for j in range(PLANE):
            if hop or j:
                pl.semaphore_signal(barrier, inc=1, **device(row_at[j], 2 * xs[hop] + core))

    across = lax.broadcasted_iota(jnp.int32, (COLS, COLS), 1)
    down = lax.broadcasted_iota(jnp.int32, (COLS, COLS), 0)

    def gram(step, ref):
        for copy in load(step):
            copy.wait()
        over_rows = (((0,), (0,)), ((), ()))
        w, q = wq[step, :, :COLS], wq[step, :, COLS:]
        gram_s = lax.dot_general(w, w, over_rows, preferred_element_type=F32)
        g = lax.dot_general(q, wq[step], over_rows, preferred_element_type=F32)
        gram_f = g[:, COLS:]
        ref[pl.ds(0, PLANE), 0:8, :] = g[:, :COLS].reshape(PLANE, 8, COLS)
        ref[pl.ds(0, PLANE), 8:16, :] = jnp.where(down >= across, gram_s, gram_f).reshape(
            PLANE, 8, COLS
        )
        diagonal = jnp.sum(jnp.where(down == across, gram_f, 0.0), axis=0, keepdims=True)
        ref[PLANE] = jnp.broadcast_to(diagonal, (16, COLS))
        if step + ahead < SYSTEMS:
            for copy in load(step + ahead):
                copy.start()

    def lend(k):
        return pltpu.make_async_remote_copy(
            src_ref=lent.at[k], dst_ref=given.at[k], send_sem=lent_sem.at[k],
            recv_sem=given_sem.at[k], **device(me_row, 2 * x + 1 - core),
        )

    def scatter(k):
        hop = (2, 1, 3, 0)[k]
        target = 2 * xs[hop] + core
        for j in range(PLANE):
            if hop or j:
                pltpu.make_async_remote_copy(
                    src_ref=sums.at[k, row_at[j]], dst_ref=arrived.at[PLANE * hop + j],
                    send_sem=send_sem, recv_sem=recv_sem, **device(row_at[j], target),
                ).start()

        def diagonal():
            pltpu.make_async_remote_copy(
                src_ref=sums.at[k, PLANE, pl.ds(0, 8)], dst_ref=diagonals.at[PLANE * hop + to_first],
                send_sem=diag_send, recv_sem=diag_recv, **device(0, target),
            ).start()

        if hop:
            diagonal()
        else:
            pl.when(me_row != 0)(diagonal)
            arrived[0] = sums[k, me_row]

            @pl.when(me_row == 0)
            def _():
                diagonals[0] = sums[k, PLANE, 0:8]

    gram(0, lent.at[0])
    pl.semaphore_wait(barrier, CHIPS - 1 + 4)
    lend(0).start()
    for k in range(4):
        gram(2 * k + 1, sums.at[k])
        if k < 3:
            gram(2 * k + 2, lent.at[k + 1])
            lend(k + 1).start()
        lend(k).wait_recv()
        sums[k] = sums[k] + given[k]
        scatter(k)

    fetch_chosen.wait()
    chosen = chosen_ref[pl.ds(me_group, 1), :]
    coeffs[...] = (lax.broadcasted_iota(jnp.int32, (COLS, KEPT), 0) == chosen).astype(F32).T

    others = arrived.at[pl.ds(1, CHIPS - 1)]
    landed(others, recv_sem)

    def add(i, total):
        return total + arrived[i]

    pieces[me_row] = lax.fori_loop(1, CHIPS, add, arrived[0], unroll=9)

    def share(j, part, send, recv):
        return pltpu.make_async_remote_copy(
            src_ref=part, dst_ref=part, send_sem=send, recv_sem=recv, **device(row_at[j], me_group)
        )

    for j in range(1, PLANE):
        share(j, pieces.at[me_row], share_send, share_recv).start()
    fifteen = pieces.at[pl.ds(0, PLANE - 1)]
    shared_diagonal = pieces.at[PLANE, pl.ds(0, 8)]

    @pl.when(me_row == 0)
    def _():
        landed(diagonals.at[pl.ds(1, CHIPS - 1)], diag_recv)
        pieces[PLANE, 0:8, :] = lax.fori_loop(
            1, CHIPS, lambda i, total: total + diagonals[i], diagonals[0], unroll=9
        )
        for j in range(1, PLANE):
            share(j, shared_diagonal, share_diag_send, share_diag_recv).start()

    @pl.when(me_row != 0)
    def _():
        landed(shared_diagonal, share_diag_recv)

    landed(fifteen, share_recv)

    sub = lax.broadcasted_iota(jnp.int32, (8, 128), 0)
    mixed = stacked([pieces[i, 8:16, :] for i in range(PLANE)])
    turned = mixed.T
    diagonal = jnp.broadcast_to(pieces[PLANE, 0:1, :], (COLS, COLS))
    gram_f = jnp.where(down < across, mixed, jnp.where(down == across, diagonal, turned))
    gram_s = jnp.where(down >= across, mixed, turned)
    step_matrix = solved(gram_f, stacked([pieces[i, 0:8, :] for i in range(PLANE)]), sub)
    moves = stacked([step_matrix, dot(gram_s, step_matrix, 1, 0)])

    def iterate(i, _):
        moved = dot(coeffs[...], moves, 1, 1)
        solution_t, weighted = moved[:, :COLS], moved[:, COLS:]
        metric = dot(solution_t, weighted, 1, 1) * (1.0 / total_rows)
        wide = jnp.concatenate([metric, jnp.zeros((KEPT, COLS - KEPT), F32)], axis=1)
        coeffs[...] = stacked(normalised_rows(tiles(wide), tiles(solution_t), sub))
        return 0

    lax.fori_loop(0, ITERS, iterate, 0)
    local_coeffs[...] = coeffs[...].astype(BF16)
    out_ref[me_group] = local_coeffs[...]
    for i in range(1, SYSTEMS):
        pltpu.make_async_remote_copy(
            src_ref=local_coeffs, dst_ref=out_ref.at[me_group], send_sem=done_send,
            recv_sem=done_recv, **device(me_row, lax.rem(me_group + i, SYSTEMS)),
        ).start()
    seven = out_ref.at[pl.ds(0, SYSTEMS - 1)]
    landed(seven, done_recv)
    landed(seven, done_send)
    landed(fifteen, share_send)
    landed(others, send_sem)
    landed(diagonals.at[pl.ds(0, 3)], diag_send)

    @pl.when(me_row != 0)
    def _():
        landed(shared_diagonal, diag_send)

    @pl.when(me_row == 0)
    def _():
        landed(diagonals.at[pl.ds(0, PLANE - 1)], share_diag_send)

    for k in range(4):
        lend(k).wait_send()


def in_hbm(a):
    return pltpu.with_memory_space_constraint(a, pltpu.HBM)


def gathered(basis, image, selection, total_rows):
    piece = (16, COLS)
    dma = pltpu.SemaphoreType.DMA
    return pl.pallas_call(
        functools.partial(gather_kernel, total_rows),
        out_shape=[
            pltpu.VMEM((SYSTEMS, KEPT, COLS), BF16),
            pltpu.VMEM((SYSTEMS, DEPTH, 2 * COLS), BF16),
        ],
        in_specs=[pl.BlockSpec(memory_space=pltpu.HBM)] * 3,
        out_specs=[pl.BlockSpec(memory_space=pltpu.VMEM)] * 2,
        scratch_shapes=[
            pltpu.VMEM((SYSTEMS, KEPT), jnp.int32),
            pltpu.VMEM((4, PLANE + 1, *piece), F32),
            pltpu.VMEM((4, PLANE + 1, *piece), F32),
            pltpu.VMEM((4, PLANE + 1, *piece), F32),
            pltpu.VMEM((CHIPS, *piece), F32),
            pltpu.VMEM((CHIPS, 8, COLS), F32),
            pltpu.VMEM((PLANE + 1, *piece), F32),
            pltpu.VMEM((KEPT, COLS), F32),
            pltpu.VMEM((KEPT, COLS), BF16),
            dma((SYSTEMS, 2)),
            dma((4,)),
            dma((4,)),
            *[dma] * 11,
        ],
        compiler_params=pltpu.CompilerParams(
            collective_id=0, has_side_effects=True, vmem_limit_bytes=40 * 2**20
        ),
        name="gather_solve",
    )(in_hbm(basis), in_hbm(image), in_hbm(selection))


def rotate_kernel(wq, c_ref, o_hbm, both, out, sem):
    group = lax.axis_index("groups")
    x, core = group // 2, lax.rem(group, 2)
    block, part = out.shape[1], 512
    per = DEPTH // block
    both[...] = jnp.zeros_like(both)

    def store(t):
        s = system_at(t // per, x, core)
        return pltpu.make_async_copy(
            out.at[t], o_hbm.at[s, pl.ds(t % per * block, block)], sem.at[t]
        )

    for t in range(SYSTEMS * per):
        step, slot = t // per, t // per % 2
        if t % per == 0:
            coeffs = c_ref[system_at(step, x, core)]
            both[slot, :KEPT, :COLS] = coeffs
            both[slot, KEPT:, COLS:] = coeffs
        for u in range(0, block, part):
            at = t % per * block + u
            out[t, u : u + part] = lax.dot_general(
                wq[step, at : at + part, :], both[slot],
                (((1,), (1,)), ((), ())), preferred_element_type=F32,
            ).astype(BF16)
        store(t).start()
    for t in range(SYSTEMS * per):
        store(t).wait()


def rotated(wq, coeffs):
    block = 2048
    blocks = SYSTEMS * DEPTH // block
    return pl.pallas_call(
        rotate_kernel,
        out_shape=jax.ShapeDtypeStruct((SYSTEMS, DEPTH, COLS), BF16),
        in_specs=[pl.BlockSpec(memory_space=pltpu.VMEM)] * 2,
        out_specs=pl.BlockSpec(memory_space=pltpu.HBM),
        scratch_shapes=[
            pltpu.VMEM((2, 2 * KEPT, 2 * COLS), BF16),
            pltpu.VMEM((blocks, block, COLS), BF16),
            pltpu.SemaphoreType.DMA((blocks,)),
        ],
        compiler_params=pltpu.CompilerParams(vmem_limit_bytes=24 * 2**20),
        name="rotate",
    )(wq, coeffs)


def on_device(basis, image, selection):
    total_rows = basis.shape[1] * lax.axis_size("rows") * lax.axis_size("groups")
    coeffs, wq = gathered(basis, image, selection, total_rows)
    return rotated(wq, coeffs)


def solution(mesh):
    in_specs = (P(None, ("rows", "groups"), None), P(None, ("rows", "groups"), None), P())
    out_specs = P(None, ("rows", "groups"), None)
    return jax.shard_map(
        on_device, mesh=mesh, in_specs=in_specs, out_specs=out_specs, check_vma=False
    )
```

time: 78.1 us -> 51.5 us (0.66)
  Pallas kernels: 72.8 us -> 51.2 us
  local copies, waits for them, and re-layouts: 4.71 us -> 0 us
    pallas_call x2, Pallas kernels: 72.8 us -> 51.2 us  [the longest x1 45.7 us: gathered(): pl.pallas_call(functools.partial(gather_kernel, total_rows), out_shape=[p...]
    unnamed x6 -> x0, local copies, waits for them, and re-layouts: 4.71 us -> none
where the time goes in v2:
time: 51.5 us; the launch traced here: 51.4 us
  Pallas kernels  51.2 us (99%)
    pallas_call x1, Pallas kernels, gathered(): pl.pallas_call(functools.partial(gather_kernel, total_rows), out_shape=[p...  45.7 us
    pallas_call x1, Pallas kernels, rotated(): pl.pallas_call(rotate_kernel, out_shape=jax.ShapeDtypeStruct((SYSTEMS, DE...  5.5 us

profile of v2, /device:TPU:1, one launch (start us, length us, event | category | flops | bytes accessed | tf_op | source)
XLA Modules:
  0.0 51.4 jit_solution(6876485045459086307)
XLA Ops:
  0.0 45.7 %gather_solve.1 = (bf16[8,64,128]{2,1,0:T(8,128)(2,1)S(1)}, bf16[8,4096,256]{2,1,0:T(8,128)(2,1)S(1)}) custom-call(bf16[8,4096,128]{2,1,0:T(8,128)(2,1)} %w_hbm.1, bf16[8,4096,128]{2,1,0:T(8,128)(2,1)} %q_hbm.1, s32[8,64]{1,0:T(8,128)} %chosen_hbm.1), custom_call_target="tpu_custom_call" | custom-call | tf_op jit(solution)/shard_map/gather_solve/pallas_call | solution.py:340
  45.7 5.5 %rotate.1 = bf16[8,4096,128]{2,1,0:T(8,128)(2,1)} custom-call(bf16[8,4096,256]{2,1,0:T(8,128)(2,1)S(1)} %get-tuple-element.7.wq, bf16[8,64,128]{2,1,0:T(8,128)(2,1)S(1)} %get-tuple-element.8.c_ref), custom_call_target="tpu_custom_call" | custom-call | tf_op jit(solution)/shard_map/rotate/pallas_call | solution.py:403

commit v3 on v2

--- a/solution.py
+++ b/solution.py
@@ -8,6 +8,8 @@
 from jax.sharding import PartitionSpec as P
 
 ITERS = 3
+EARLY = 1
+TURNED = 4
 F32 = jnp.float32
 BF16 = jnp.bfloat16
 SYSTEMS = 8
@@ -60,13 +62,19 @@
     return tile - added([cols[j] * rows[j] for j in range(8)])
 
 
-def pivot(v, j, at, r):
-    piv = v[j]
+def pivot_pair(v, j, sub):
+    at, at_next = sub == j, sub == j + 1
+    a, b1, b2, c = row(v[j], j), row(v[j + 1], j), row(v[j], j + 1), row(v[j + 1], j + 1)
+    r = 1.0 / (a * c - b1 * b2)
+    p = jnp.where(at, -1.0, jnp.where(at_next, 0.0, v[j]))
+    q = jnp.where(at_next, -1.0, jnp.where(at, 0.0, v[j + 1]))
+    v[j], v[j + 1] = r * (q * b2 - p * c), r * (p * b1 - q * a)
     for other in range(8):
-        if other != j:
-            w = row(v[other], j) * r
-            v[other] = jnp.where(at, w, v[other] - piv * w)
-    v[j] = jnp.where(at, r, -(piv * r))
+        if other not in (j, j + 1):
+            u, t = row(v[other], j), row(v[other], j + 1)
+            moved = p * (c * u - b1 * t) + q * (a * t - b2 * u)
+            v[other] = jnp.where(at | at_next, 0.0, v[other]) - r * moved
+    return a, b1, b2, c, r
 
 
 def stacked(parts):
@@ -84,8 +92,8 @@
             i: [lane(f[i], start + 8 * k + j) for j in range(8)]
             for i in [*range(k + 1, 8), *range(k)]
         }
-        for j in range(8):
-            pivot(v, j, sub == j, 1.0 / row(v[j], j))
+        for j in range(0, 8, 2):
+            pivot_pair(v, j, sub)
         fk, xk = times(v, f[k]), times(v, x[k])
         fr = [row(fk, j) for j in range(8)]
         xr = [row(xk, j) for j in range(8)]
@@ -119,13 +127,17 @@
         cols = {i: [lane(m[i], 8 * k + j) for j in range(8)] for i in range(k + 1, n)}
         mine = y[k]
         scale = jnp.zeros((8, 128), F32)
-        for j in range(8):
-            p = row(v[j], j)
-            r = 1.0 / p
-            at = sub == j
-            scale = jnp.where(at, p, scale)
-            mine = mine - jnp.where(sub > j, v[j] * r, 0.0) * row(mine, j)
-            pivot(v, j, at, r)
+        for j in range(0, 8, 2):
+            p, q = v[j], v[j + 1]
+            a, b1, b2, c, r = pivot_pair(v, j, sub)
+            inverse_a = 1.0 / a
+            g, h = row(mine, j), row(mine, j + 1)
+            below = r * (p * (c * g - b1 * h) + q * (a * h - b2 * g))
+            mine = mine - jnp.where(
+                sub > j + 1, below, jnp.where(sub == j + 1, (b2 * inverse_a) * g, 0.0)
+            )
+            second = (a * c - b1 * b2) * inverse_a
+            scale = jnp.where(sub == j, a, jnp.where(sub == j + 1, second, scale))
         out.append(mine * lax.rsqrt(scale))
         if k < n - 1:
             mk, yk = times(v, m[k]), times(v, y[k])
@@ -137,14 +149,33 @@
     return out
 
 
+def unit_scale(m):
+    on = lax.broadcasted_iota(jnp.int32, m.shape, 0) == lax.broadcasted_iota(jnp.int32, m.shape, 1)
+    diagonal = jnp.where(on, m, 0.0)
+    return [lax.rsqrt(jnp.sum(diagonal, axis=axis, keepdims=True)) for axis in (1, 0)]
+
+
 def system_at(step, x, core):
     hop = (2, 1, 3, 0)[step // 2]
     return 2 * lax.rem(x + hop, 4) + (1 - core if step % 2 == 0 else core)
 
 
+ROTATION_ORDER = (7, 6, 5, 4, 3, 2, 1, 0)
+
+
+def rotate(both, coeffs, data, out):
+    part = 512
+    both[:KEPT, :COLS] = coeffs
+    both[KEPT:, COLS:] = coeffs
+    for at in range(0, DEPTH, part):
+        out[at : at + part] = lax.dot_general(
+            data[at : at + part], both[...], (((1,), (1,)), ((), ())), preferred_element_type=F32
+        ).astype(BF16)
+
+
 def gather_kernel(
-    total_rows, w_hbm, q_hbm, chosen_hbm, out_ref, wq,
-    chosen_ref, lent, given, sums, arrived, diagonals, pieces, coeffs, local_coeffs,
+    total_rows, w_hbm, q_hbm, chosen_hbm, out_ref, wq, turned,
+    both, chosen_ref, lent, given, sums, arrived, diagonals, pieces, coeffs, local_coeffs,
     load_sem, lent_sem, given_sem, send_sem, recv_sem, diag_send, diag_recv,
     share_send, share_recv, share_diag_send, share_diag_recv, done_send, done_recv, chosen_sem,
 ):
@@ -237,17 +268,27 @@
             def _():
                 diagonals[0] = sums[k, PLANE, 0:8]
 
-    gram(0, lent.at[0])
-    pl.semaphore_wait(barrier, CHIPS - 1 + 4)
-    lend(0).start()
-    for k in range(4):
-        gram(2 * k + 1, sums.at[k])
-        if k < 3:
-            gram(2 * k + 2, lent.at[k + 1])
-            lend(k + 1).start()
+    def partial_gram(step):
+        gram(step, (lent if step % 2 == 0 else sums).at[step // 2])
+
+    def combine(k):
         lend(k).wait_recv()
         sums[k] = sums[k] + given[k]
         scatter(k)
+
+    for step in range(EARLY):
+        partial_gram(step)
+    pl.semaphore_wait(barrier, CHIPS - 1 + 4)
+    lent_out = combined = 0
+    for step in range(EARLY, SYSTEMS + 1):
+        while 2 * lent_out < step:
+            lend(lent_out).start()
+            lent_out += 1
+        if step < SYSTEMS:
+            partial_gram(step)
+        while 2 * combined + 1 < step:
+            combine(combined)
+            combined += 1
 
     fetch_chosen.wait()
     chosen = chosen_ref[pl.ds(me_group, 1), :]
@@ -288,32 +329,47 @@
 
     sub = lax.broadcasted_iota(jnp.int32, (8, 128), 0)
     mixed = stacked([pieces[i, 8:16, :] for i in range(PLANE)])
-    turned = mixed.T
+    mixed_t = mixed.T
     diagonal = jnp.broadcast_to(pieces[PLANE, 0:1, :], (COLS, COLS))
-    gram_f = jnp.where(down < across, mixed, jnp.where(down == across, diagonal, turned))
-    gram_s = jnp.where(down >= across, mixed, turned)
-    step_matrix = solved(gram_f, stacked([pieces[i, 0:8, :] for i in range(PLANE)]), sub)
+    gram_f = jnp.where(down < across, mixed, jnp.where(down == across, diagonal, mixed_t))
+    gram_s = jnp.where(down >= across, mixed, mixed_t)
+    by_row, by_col = unit_scale(gram_f)
+    cross_t = stacked([pieces[i, 0:8, :] for i in range(PLANE)])
+    step_matrix = solved(gram_f * by_row * by_col, cross_t * by_row, sub) * by_row
     moves = stacked([step_matrix, dot(gram_s, step_matrix, 1, 0)])
 
     def iterate(i, _):
         moved = dot(coeffs[...], moves, 1, 1)
         solution_t, weighted = moved[:, :COLS], moved[:, COLS:]
         metric = dot(solution_t, weighted, 1, 1) * (1.0 / total_rows)
+        by_row, by_col = unit_scale(metric)
+        metric = metric * by_row * by_col
         wide = jnp.concatenate([metric, jnp.zeros((KEPT, COLS - KEPT), F32)], axis=1)
-        coeffs[...] = stacked(normalised_rows(tiles(wide), tiles(solution_t), sub))
+        coeffs[...] = stacked(normalised_rows(tiles(wide), tiles(solution_t * by_row), sub))
         return 0
 
     lax.fori_loop(0, ITERS, iterate, 0)
     local_coeffs[...] = coeffs[...].astype(BF16)
     out_ref[me_group] = local_coeffs[...]
-    for i in range(1, SYSTEMS):
-        pltpu.make_async_remote_copy(
+    both[...] = jnp.zeros_like(both)
+
+    def tell(hop, same):
+        target = 2 * xs[hop] + (core if same else 1 - core)
+        return pltpu.make_async_remote_copy(
             src_ref=local_coeffs, dst_ref=out_ref.at[me_group], send_sem=done_send,
-            recv_sem=done_recv, **device(me_row, lax.rem(me_group + i, SYSTEMS)),
-        ).start()
-    seven = out_ref.at[pl.ds(0, SYSTEMS - 1)]
-    landed(seven, done_recv)
-    landed(seven, done_send)
+            recv_sem=done_recv.at[2 * hop + same], **device(me_row, target),
+        )
+
+    for hop, same in ((2, 1), (2, 0), (1, 1), (1, 0), (3, 1), (3, 0), (0, 0)):
+        tell(hop, same).start()
+    for i, step in enumerate(ROTATION_ORDER):
+        hop, same = (2, 1, 3, 0)[step // 2], step % 2
+        s = system_at(step, x, core)
+        if step != 7:
+            landed(out_ref.at[s], done_recv.at[2 * ((4 - hop) % 4) + same])
+        if i < TURNED:
+            rotate(both.at[i % 2], out_ref[s], wq.at[step], turned.at[i])
+    landed(out_ref.at[pl.ds(0, SYSTEMS - 1)], done_send)
     landed(fifteen, share_send)
     landed(others, send_sem)
     landed(diagonals.at[pl.ds(0, 3)], diag_send)
@@ -342,10 +398,12 @@
         out_shape=[
             pltpu.VMEM((SYSTEMS, KEPT, COLS), BF16),
             pltpu.VMEM((SYSTEMS, DEPTH, 2 * COLS), BF16),
+            pltpu.VMEM((TURNED, DEPTH, COLS), BF16),
         ],
         in_specs=[pl.BlockSpec(memory_space=pltpu.HBM)] * 3,
-        out_specs=[pl.BlockSpec(memory_space=pltpu.VMEM)] * 2,
+        out_specs=[pl.BlockSpec(memory_space=pltpu.VMEM)] * 3,
         scratch_shapes=[
+            pltpu.VMEM((2, 2 * KEPT, 2 * COLS), BF16),
             pltpu.VMEM((SYSTEMS, KEPT), jnp.int32),
             pltpu.VMEM((4, PLANE + 1, *piece), F32),
             pltpu.VMEM((4, PLANE + 1, *piece), F32),
@@ -358,67 +416,58 @@
             dma((SYSTEMS, 2)),
             dma((4,)),
             dma((4,)),
-            *[dma] * 11,
+            *[dma] * 9,
+            dma((SYSTEMS,)),
+            dma,
         ],
         compiler_params=pltpu.CompilerParams(
-            collective_id=0, has_side_effects=True, vmem_limit_bytes=40 * 2**20
+            collective_id=0, has_side_effects=True, vmem_limit_bytes=16 * 2**20
         ),
         name="gather_solve",
     )(in_hbm(basis), in_hbm(image), in_hbm(selection))
 
 
-def rotate_kernel(wq, c_ref, o_hbm, both, out, sem):
+def rotate_kernel(wq, turned, c_ref, o_hbm, both, out, sem):
     group = lax.axis_index("groups")
     x, core = group // 2, lax.rem(group, 2)
-    block, part = out.shape[1], 512
-    per = DEPTH // block
+
+    def store(i):
+        source = turned.at[i] if i < TURNED else out.at[i - TURNED]
+        return pltpu.make_async_copy(
+            source, o_hbm.at[system_at(ROTATION_ORDER[i], x, core)], sem.at[i]
+        )
+
+    for i in range(TURNED):
+        store(i).start()
     both[...] = jnp.zeros_like(both)
-
-    def store(t):
-        s = system_at(t // per, x, core)
-        return pltpu.make_async_copy(
-            out.at[t], o_hbm.at[s, pl.ds(t % per * block, block)], sem.at[t]
-        )
-
-    for t in range(SYSTEMS * per):
-        step, slot = t // per, t // per % 2
-        if t % per == 0:
-            coeffs = c_ref[system_at(step, x, core)]
-            both[slot, :KEPT, :COLS] = coeffs
-            both[slot, KEPT:, COLS:] = coeffs
-        for u in range(0, block, part):
-            at = t % per * block + u
-            out[t, u : u + part] = lax.dot_general(
-                wq[step, at : at + part, :], both[slot],
-                (((1,), (1,)), ((), ())), preferred_element_type=F32,
-            ).astype(BF16)
-        store(t).start()
-    for t in range(SYSTEMS * per):
-        store(t).wait()
-
-
-def rotated(wq, coeffs):
-    block = 2048
-    blocks = SYSTEMS * DEPTH // block
+    for i in range(TURNED, SYSTEMS):
+        step = ROTATION_ORDER[i]
+        coeffs = c_ref[system_at(step, x, core)]
+        rotate(both.at[i % 2], coeffs, wq.at[step], out.at[i - TURNED])
+        store(i).start()
+    for i in range(SYSTEMS):
+        store(i).wait()
+
+
+def rotated(coeffs, wq, turned):
     return pl.pallas_call(
         rotate_kernel,
         out_shape=jax.ShapeDtypeStruct((SYSTEMS, DEPTH, COLS), BF16),
-        in_specs=[pl.BlockSpec(memory_space=pltpu.VMEM)] * 2,
+        in_specs=[pl.BlockSpec(memory_space=pltpu.VMEM)] * 3,
         out_specs=pl.BlockSpec(memory_space=pltpu.HBM),
         scratch_shapes=[
             pltpu.VMEM((2, 2 * KEPT, 2 * COLS), BF16),
-            pltpu.VMEM((blocks, block, COLS), BF16),
-            pltpu.SemaphoreType.DMA((blocks,)),
+            pltpu.VMEM((SYSTEMS - TURNED, DEPTH, COLS), BF16),
+            pltpu.SemaphoreType.DMA((SYSTEMS,)),
         ],
-        compiler_params=pltpu.CompilerParams(vmem_limit_bytes=24 * 2**20),
+        compiler_params=pltpu.CompilerParams(vmem_limit_bytes=16 * 2**20),
         name="rotate",
-    )(wq, coeffs)
+    )(wq, turned, coeffs)
 
 
 def on_device(basis, image, selection):
     total_rows = basis.shape[1] * lax.axis_size("rows") * lax.axis_size("groups")
-    coeffs, wq = gathered(basis, image, selection, total_rows)
-    return rotated(wq, coeffs)
+    return rotated(*gathered(basis, image, selection, total_rows))
 
 
 def solution(mesh):

time: 51.5 us -> 47.1 us (0.915)
  Pallas kernels: 51.2 us -> 46.9 us
    pallas_call x1, Pallas kernels: 45.7 us -> 43.4 us  [gathered(): pl.pallas_call(functools.partial(gather_kernel, total_rows), out_shape=[p...]
    pallas_call x1, Pallas kernels: 5.5 us -> 3.41 us  [rotated(): pl.pallas_call(rotate_kernel, out_shape=jax.ShapeDtypeStruct((SYSTEMS, DE...]
where the time goes in v3:
time: 47.1 us; the launch traced here: 47 us
  Pallas kernels  46.9 us (100%)
    pallas_call x1, Pallas kernels, gathered(): pl.pallas_call(functools.partial(gather_kernel, total_rows), out_shape=[p...  43.4 us
    pallas_call x1, Pallas kernels, rotated(): pl.pallas_call(rotate_kernel, out_shape=jax.ShapeDtypeStruct((SYSTEMS, DE...  3.41 us

profile of v3, /device:TPU:1, one launch (start us, length us, event | category | flops | bytes accessed | tf_op | source)
XLA Modules:
  0.0 47.0 jit_solution(16070733934866824052)
XLA Ops:
  0.0 43.4 %gather_solve.1 = (bf16[8,64,128]{2,1,0:T(8,128)(2,1)S(1)}, bf16[8,4096,256]{2,1,0:T(8,128)(2,1)S(1)}, bf16[4,4096,128]{2,1,0:T(8,128)(2,1)S(1)}) custom-call(bf16[8,4096,128]{2,1,0:T(8,128)(2,1)} %w_hbm.1, bf16[8,4096,128]{2,1,0:T(8,128)(2,1)} %q_hbm.1, s32[8,64]{1,0:T(8,128)} %chosen_hbm.1), custom_call_target="tpu_custom_call" | custom-call | tf_op jit(solution)/shard_map/gather_solve/pallas_call | solution.py:396
  43.5 3.4 %rotate.1 = bf16[8,4096,128]{2,1,0:T(8,128)(2,1)} custom-call(bf16[8,4096,256]{2,1,0:T(8,128)(2,1)S(1)} %get-tuple-element.8.wq, bf16[4,4096,128]{2,1,0:T(8,128)(2,1)S(1)} %get-tuple-element.9.turned, bf16[8,64,128]{2,1,0:T(8,128)(2,1)S(1)} %get-tuple-element.10.c_ref), custom_call_target="tpu_custom_call" | custom-call | tf_op jit(solution)/shard_map/rotate/pallas_call | solution.py:453

commit v4 on v3

--- a/solution.py
+++ b/solution.py
@@ -8,7 +8,6 @@
 from jax.sharding import PartitionSpec as P
 
 ITERS = 3
-EARLY = 1
 TURNED = 4
 F32 = jnp.float32
 BF16 = jnp.bfloat16
@@ -16,7 +15,6 @@
 DEPTH = 4096
 COLS = 128
 KEPT = 64
-CHIPS = 64
 PLANE = 16
 
 
@@ -155,12 +153,19 @@
     return [lax.rsqrt(jnp.sum(diagonal, axis=axis, keepdims=True)) for axis in (1, 0)]
 
 
+HOPS = (2, 0, 1, 3)
+ORDER = ((0, 0), (1, 0), (0, 1), (2, 0), (1, 1), (3, 0), (2, 1), (3, 1))
+AHEAD = 4
+LANDING = {0: 0, 1: 1, 3: 2}
+SENDERS = 3 * PLANE
+
+
 def system_at(step, x, core):
-    hop = (2, 1, 3, 0)[step // 2]
-    return 2 * lax.rem(x + hop, 4) + (1 - core if step % 2 == 0 else core)
-
-
-ROTATION_ORDER = (7, 6, 5, 4, 3, 2, 1, 0)
+    k, own = ORDER[step]
+    return 2 * lax.rem(x + HOPS[k], 4) + (core if own else 1 - core)
+
+
+ROTATION_ORDER = tuple(ORDER.index(c) for c in ((1, 1), (1, 0), (2, 1), (2, 0), (3, 1), (3, 0), (0, 1), (0, 0)))
 
 
 def rotate(both, coeffs, data, out):
@@ -175,8 +180,8 @@
 
 def gather_kernel(
     total_rows, w_hbm, q_hbm, chosen_hbm, out_ref, wq, turned,
-    both, chosen_ref, lent, given, sums, arrived, diagonals, pieces, coeffs, local_coeffs,
-    load_sem, lent_sem, given_sem, send_sem, recv_sem, diag_send, diag_recv,
+    both, chosen_ref, lent, given, sums, relayed, arrived, diagonals, pieces, coeffs, local_coeffs,
+    load_sem, lent_sem, given_sem, relay_send, relay_recv, send_sem, recv_sem, diag_send, diag_recv,
     share_send, share_recv, share_diag_send, share_diag_recv, done_send, done_recv, chosen_sem,
 ):
     me_row, me_group = lax.axis_index("rows"), lax.axis_index("groups")
@@ -201,8 +206,7 @@
             for i, (ref, off) in enumerate(((w_hbm, 0), (q_hbm, COLS)))
         ]
 
-    ahead = 4
-    for step in range(ahead):
+    for step in range(AHEAD):
         for copy in load(step):
             copy.start()
     fetch_chosen = pltpu.make_async_copy(chosen_hbm, chosen_ref, chosen_sem)
@@ -211,7 +215,7 @@
     barrier = pltpu.get_barrier_semaphore()
     for hop in range(4):
         pl.semaphore_signal(barrier, inc=1, **device(me_row, 2 * xs[hop] + 1 - core))
-        for j in range(PLANE):
+        for j in range(PLANE if hop != 2 else 1):
             if hop or j:
                 pl.semaphore_signal(barrier, inc=1, **device(row_at[j], 2 * xs[hop] + core))
 
@@ -232,8 +236,8 @@
         )
         diagonal = jnp.sum(jnp.where(down == across, gram_f, 0.0), axis=0, keepdims=True)
         ref[PLANE] = jnp.broadcast_to(diagonal, (16, COLS))
-        if step + ahead < SYSTEMS:
-            for copy in load(step + ahead):
+        if step + AHEAD < SYSTEMS:
+            for copy in load(step + AHEAD):
                 copy.start()
 
     def lend(k):
@@ -243,18 +247,18 @@
         )
 
     def scatter(k):
-        hop = (2, 1, 3, 0)[k]
+        hop = HOPS[k]
         target = 2 * xs[hop] + core
         for j in range(PLANE):
             if hop or j:
                 pltpu.make_async_remote_copy(
-                    src_ref=sums.at[k, row_at[j]], dst_ref=arrived.at[PLANE * hop + j],
+                    src_ref=sums.at[k, row_at[j]], dst_ref=arrived.at[PLANE * LANDING[hop] + j],
                     send_sem=send_sem, recv_sem=recv_sem, **device(row_at[j], target),
                 ).start()
 
         def diagonal():
             pltpu.make_async_remote_copy(
-                src_ref=sums.at[k, PLANE, pl.ds(0, 8)], dst_ref=diagonals.at[PLANE * hop + to_first],
+                src_ref=sums.at[k, PLANE, pl.ds(0, 8)], dst_ref=diagonals.at[PLANE * LANDING[hop] + to_first],
                 send_sem=diag_send, recv_sem=diag_recv, **device(0, target),
             ).start()
 
@@ -268,39 +272,48 @@
             def _():
                 diagonals[0] = sums[k, PLANE, 0:8]
 
-    def partial_gram(step):
-        gram(step, (lent if step % 2 == 0 else sums).at[step // 2])
+    halves = {3: pl.ds(0, PLANE // 2), 1: pl.ds(PLANE // 2, PLANE // 2 + 1)}
+
+    def relay(hop):
+        return pltpu.make_async_remote_copy(
+            src_ref=sums.at[0, halves[hop]], dst_ref=relayed.at[halves[hop]],
+            send_sem=relay_send.at[hop], recv_sem=relay_recv.at[hop],
+            **device(me_row, 2 * xs[hop] + core),
+        )
 
     def combine(k):
+        hop = HOPS[k]
         lend(k).wait_recv()
         sums[k] = sums[k] + given[k]
+        if hop == 2:
+            relay(1).start()
+            relay(3).start()
+            return
+        if hop:
+            relay(hop).wait_recv()
+            sums[k, halves[hop]] = sums[k, halves[hop]] + relayed[halves[hop]]
         scatter(k)
 
-    for step in range(EARLY):
-        partial_gram(step)
-    pl.semaphore_wait(barrier, CHIPS - 1 + 4)
-    lent_out = combined = 0
-    for step in range(EARLY, SYSTEMS + 1):
-        while 2 * lent_out < step:
-            lend(lent_out).start()
-            lent_out += 1
-        if step < SYSTEMS:
-            partial_gram(step)
-        while 2 * combined + 1 < step:
-            combine(combined)
-            combined += 1
+    for step, (k, own) in enumerate(ORDER):
+        gram(step, (sums if own else lent).at[k])
+        if step == 0:
+            pl.semaphore_wait(barrier, SENDERS - 1 + 5)
+        if own:
+            combine(k)
+        else:
+            lend(k).start()
 
     fetch_chosen.wait()
     chosen = chosen_ref[pl.ds(me_group, 1), :]
     coeffs[...] = (lax.broadcasted_iota(jnp.int32, (COLS, KEPT), 0) == chosen).astype(F32).T
 
-    others = arrived.at[pl.ds(1, CHIPS - 1)]
+    others = arrived.at[pl.ds(1, SENDERS - 1)]
     landed(others, recv_sem)
 
     def add(i, total):
         return total + arrived[i]
 
-    pieces[me_row] = lax.fori_loop(1, CHIPS, add, arrived[0], unroll=9)
+    pieces[me_row] = lax.fori_loop(1, SENDERS, add, arrived[0], unroll=47)
 
     def share(j, part, send, recv):
         return pltpu.make_async_remote_copy(
@@ -314,9 +327,9 @@
 
     @pl.when(me_row == 0)
     def _():
-        landed(diagonals.at[pl.ds(1, CHIPS - 1)], diag_recv)
+        landed(diagonals.at[pl.ds(1, SENDERS - 1)], diag_recv)
         pieces[PLANE, 0:8, :] = lax.fori_loop(
-            1, CHIPS, lambda i, total: total + diagonals[i], diagonals[0], unroll=9
+            1, SENDERS, lambda i, total: total + diagonals[i], diagonals[0], unroll=47
         )
         for j in range(1, PLANE):
             share(j, shared_diagonal, share_diag_send, share_diag_recv).start()
@@ -363,16 +376,17 @@
     for hop, same in ((2, 1), (2, 0), (1, 1), (1, 0), (3, 1), (3, 0), (0, 0)):
         tell(hop, same).start()
     for i, step in enumerate(ROTATION_ORDER):
-        hop, same = (2, 1, 3, 0)[step // 2], step % 2
+        k, same = ORDER[step]
+        hop = HOPS[k]
         s = system_at(step, x, core)
-        if step != 7:
+        if i:
             landed(out_ref.at[s], done_recv.at[2 * ((4 - hop) % 4) + same])
         if i < TURNED:
             rotate(both.at[i % 2], out_ref[s], wq.at[step], turned.at[i])
     landed(out_ref.at[pl.ds(0, SYSTEMS - 1)], done_send)
     landed(fifteen, share_send)
     landed(others, send_sem)
-    landed(diagonals.at[pl.ds(0, 3)], diag_send)
+    landed(diagonals.at[pl.ds(0, 2)], diag_send)
 
     @pl.when(me_row != 0)
     def _():
@@ -384,6 +398,8 @@
 
     for k in range(4):
         lend(k).wait_send()
+    relay(1).wait_send()
+    relay(3).wait_send()
 
 
 def in_hbm(a):
@@ -408,12 +424,15 @@
             pltpu.VMEM((4, PLANE + 1, *piece), F32),
             pltpu.VMEM((4, PLANE + 1, *piece), F32),
             pltpu.VMEM((4, PLANE + 1, *piece), F32),
-            pltpu.VMEM((CHIPS, *piece), F32),
-            pltpu.VMEM((CHIPS, 8, COLS), F32),
+            pltpu.VMEM((PLANE + 1, *piece), F32),
+            pltpu.VMEM((SENDERS, *piece), F32),
+            pltpu.VMEM((SENDERS, 8, COLS), F32),
             pltpu.VMEM((PLANE + 1, *piece), F32),
             pltpu.VMEM((KEPT, COLS), F32),
             pltpu.VMEM((KEPT, COLS), BF16),
             dma((SYSTEMS, 2)),
+            dma((4,)),
+            dma((4,)),
             dma((4,)),
             dma((4,)),
             *[dma] * 9,

time: 47.1 us -> 45.8 us (0.972)
  Pallas kernels: 46.9 us -> 45.5 us
    pallas_call x1, Pallas kernels: 43.4 us -> 42.1 us  [gathered(): pl.pallas_call(functools.partial(gather_kernel, total_rows), out_shape=[p...]
where the time goes in v4:
time: 45.8 us; the launch traced here: 45.7 us
  Pallas kernels  45.5 us (99%)
    pallas_call x1, Pallas kernels, gathered(): pl.pallas_call(functools.partial(gather_kernel, total_rows), out_shape=[p...  42.1 us
    pallas_call x1, Pallas kernels, rotated(): pl.pallas_call(rotate_kernel, out_shape=jax.ShapeDtypeStruct((SYSTEMS, DE...  3.41 us

profile of v4, /device:TPU:1, one launch (start us, length us, event | category | flops | bytes accessed | tf_op | source)
XLA Modules:
  0.0 45.7 jit_solution(12136771175068657973)
XLA Ops:
  0.0 42.1 %gather_solve.1 = (bf16[8,64,128]{2,1,0:T(8,128)(2,1)S(1)}, bf16[8,4096,256]{2,1,0:T(8,128)(2,1)S(1)}, bf16[4,4096,128]{2,1,0:T(8,128)(2,1)S(1)}) custom-call(bf16[8,4096,128]{2,1,0:T(8,128)(2,1)} %w_hbm.1, bf16[8,4096,128]{2,1,0:T(8,128)(2,1)} %q_hbm.1, s32[8,64]{1,0:T(8,128)} %chosen_hbm.1), custom_call_target="tpu_custom_call" | custom-call | tf_op jit(solution)/shard_map/gather_solve/pallas_call | solution.py:412
  42.1 3.4 %rotate.1 = bf16[8,4096,128]{2,1,0:T(8,128)(2,1)} custom-call(bf16[8,4096,256]{2,1,0:T(8,128)(2,1)S(1)} %get-tuple-element.8.wq, bf16[4,4096,128]{2,1,0:T(8,128)(2,1)S(1)} %get-tuple-element.9.turned, bf16[8,64,128]{2,1,0:T(8,128)(2,1)S(1)} %get-tuple-element.10.c_ref), custom_call_target="tpu_custom_call" | custom-call | tf_op jit(solution)/shard_map/rotate/pallas_call | solution.py:472

commit v5 on v4

--- a/solution.py
+++ b/solution.py
@@ -117,12 +117,21 @@
     return stacked([xt - dot(jnp.where(left, 0.0, ft), stacked([zero, xl]), 1, 0), xl])
 
 
+def next_block(inverse, raw, below):
+    g = [added([below[m] * row(inverse[j], m) for m in range(8)]) for j in range(8)]
+    return [raw[i] - added([g[j] * row(below[j], i) for j in range(8)]) for i in range(8)]
+
+
 def normalised_rows(m, y, sub):
     n = len(m)
     out = []
+    v = [lane(m[0], j) + 0.0 for j in range(8)]
     for k in range(n):
-        v = [lane(m[k], 8 * k + j) + 0.0 for j in range(8)]
+        if k < n - 1:
+            raw = [lane(m[k + 1], 8 * k + 8 + j) + 0.0 for j in range(8)]
         cols = {i: [lane(m[i], 8 * k + j) for j in range(8)] for i in range(k + 1, n)}
+        if k < n - 1:
+            cols[k + 1] = [c + 0.0 for c in cols[k + 1]]
         mine = y[k]
         scale = jnp.zeros((8, 128), F32)
         for j in range(0, 8, 2):
@@ -138,7 +147,9 @@
             scale = jnp.where(sub == j, a, jnp.where(sub == j + 1, second, scale))
         out.append(mine * lax.rsqrt(scale))
         if k < n - 1:
-            mk, yk = times(v, m[k]), times(v, y[k])
+            inverse = v
+            v = next_block(inverse, raw, cols[k + 1])
+            mk, yk = times(inverse, m[k]), times(inverse, y[k])
             mr = [row(mk, j) for j in range(8)]
             yr = [row(yk, j) for j in range(8)]
             for i in cols:
@@ -225,6 +236,9 @@
     def gram(step, ref):
         for copy in load(step):
             copy.wait()
+        if step + AHEAD < SYSTEMS:
+            for copy in load(step + AHEAD):
+                copy.start()
         over_rows = (((0,), (0,)), ((), ()))
         w, q = wq[step, :, :COLS], wq[step, :, COLS:]
         gram_s = lax.dot_general(w, w, over_rows, preferred_element_type=F32)
@@ -236,9 +250,6 @@
         )
         diagonal = jnp.sum(jnp.where(down == across, gram_f, 0.0), axis=0, keepdims=True)
         ref[PLANE] = jnp.broadcast_to(diagonal, (16, COLS))
-        if step + AHEAD < SYSTEMS:
-            for copy in load(step + AHEAD):
-                copy.start()
 
     def lend(k):
         return pltpu.make_async_remote_copy(
@@ -346,7 +357,7 @@
     diagonal = jnp.broadcast_to(pieces[PLANE, 0:1, :], (COLS, COLS))
     gram_f = jnp.where(down < across, mixed, jnp.where(down == across, diagonal, mixed_t))
     gram_s = jnp.where(down >= across, mixed, mixed_t)
-    by_row, by_col = unit_scale(gram_f)
+    by_row, by_col = unit_scale(diagonal)
     cross_t = stacked([pieces[i, 0:8, :] for i in range(PLANE)])
     step_matrix = solved(gram_f * by_row * by_col, cross_t * by_row, sub) * by_row
     moves = stacked([step_matrix, dot(gram_s, step_matrix, 1, 0)])

time: 45.8 us -> 44.4 us (0.969)
  Pallas kernels: 45.5 us -> 44.1 us
    pallas_call x1, Pallas kernels: 42.1 us -> 40.7 us  [gathered(): pl.pallas_call(functools.partial(gather_kernel, total_rows), out_shape=[p...]
where the time goes in v5:
time: 44.4 us; the launch traced here: 44.3 us
  Pallas kernels  44.1 us (99%)
    pallas_call x1, Pallas kernels, gathered(): pl.pallas_call(functools.partial(gather_kernel, total_rows), out_shape=[p...  40.7 us
    pallas_call x1, Pallas kernels, rotated(): pl.pallas_call(rotate_kernel, out_shape=jax.ShapeDtypeStruct((SYSTEMS, DE...  3.41 us

profile of v5, /device:TPU:1, one launch (start us, length us, event | category | flops | bytes accessed | tf_op | source)
XLA Modules:
  0.0 44.3 jit_solution(11753011766303895142)
XLA Ops:
  0.0 40.7 %gather_solve.1 = (bf16[8,64,128]{2,1,0:T(8,128)(2,1)S(1)}, bf16[8,4096,256]{2,1,0:T(8,128)(2,1)S(1)}, bf16[4,4096,128]{2,1,0:T(8,128)(2,1)S(1)}) custom-call(bf16[8,4096,128]{2,1,0:T(8,128)(2,1)} %w_hbm.1, bf16[8,4096,128]{2,1,0:T(8,128)(2,1)} %q_hbm.1, s32[8,64]{1,0:T(8,128)} %chosen_hbm.1), custom_call_target="tpu_custom_call" | custom-call | tf_op jit(solution)/shard_map/gather_solve/pallas_call | solution.py:423
  40.7 3.4 %rotate.1 = bf16[8,4096,128]{2,1,0:T(8,128)(2,1)} custom-call(bf16[8,4096,256]{2,1,0:T(8,128)(2,1)S(1)} %get-tuple-element.8.wq, bf16[4,4096,128]{2,1,0:T(8,128)(2,1)S(1)} %get-tuple-element.9.turned, bf16[8,64,128]{2,1,0:T(8,128)(2,1)S(1)} %get-tuple-element.10.c_ref), custom_call_target="tpu_custom_call" | custom-call | tf_op jit(solution)/shard_map/rotate/pallas_call | solution.py:483

commit v6 on v5

--- a/solution.py
+++ b/solution.py
@@ -25,17 +25,20 @@
     return high, middle, (rest - middle.astype(F32)).astype(BF16)
 
 
-def dot(a, b, over_a, over_b):
+def right_parts(b, over_b):
+    b1, b2, b3 = split(b)
+    return [jnp.concatenate(pair, axis=over_b) for pair in ((b1, b1), (b2, b2), (b3, b1))]
+
+
+def dot(a, b, over_a, over_b, parts=None):
     dims = (((over_a,), (over_b,)), ((), ()))
-
-    def both(p, q, r, s):
-        return lax.dot_general(
-            jnp.concatenate([p, q], axis=over_a), jnp.concatenate([r, s], axis=over_b), dims,
-            preferred_element_type=F32,
-        )
-
-    (a1, a2, a3), (b1, b2, b3) = split(a), split(b)
-    return both(a1, a2, b1, b1) + (both(a1, a2, b2, b2) + both(a1, a3, b3, b1))
+    a1, a2, a3 = split(a)
+    a12, a13 = (jnp.concatenate([a1, other], axis=over_a) for other in (a2, a3))
+    terms = [
+        lax.dot_general(left, right, dims, preferred_element_type=F32)
+        for left, right in zip((a12, a12, a13), parts or right_parts(b, over_b))
+    ]
+    return terms[0] + (terms[1] + terms[2])
 
 
 def lane(tile, j):
@@ -167,6 +170,7 @@
 HOPS = (2, 0, 1, 3)
 ORDER = ((0, 0), (1, 0), (0, 1), (2, 0), (1, 1), (3, 0), (2, 1), (3, 1))
 AHEAD = 4
+FAR_FIRST = sorted(range(PLANE), key=lambda j: -sum((0, 1, 2, 1)[c] for c in (j // 4, j % 4)))
 LANDING = {0: 0, 1: 1, 3: 2}
 SENDERS = 3 * PLANE
 
@@ -191,7 +195,7 @@
 
 def gather_kernel(
     total_rows, w_hbm, q_hbm, chosen_hbm, out_ref, wq, turned,
-    both, chosen_ref, lent, given, sums, relayed, arrived, diagonals, pieces, coeffs, local_coeffs,
+    both, chosen_ref, lent, given, sums, relayed, arrived, diagonals, pieces, moves_ref, coeffs, local_coeffs,
     load_sem, lent_sem, given_sem, relay_send, relay_recv, send_sem, recv_sem, diag_send, diag_recv,
     share_send, share_recv, share_diag_send, share_diag_recv, done_send, done_recv, chosen_sem,
 ):
@@ -260,28 +264,29 @@
     def scatter(k):
         hop = HOPS[k]
         target = 2 * xs[hop] + core
-        for j in range(PLANE):
+
+        def diagonal():
+            pltpu.make_async_remote_copy(
+                src_ref=sums.at[k, PLANE, pl.ds(0, 8)], dst_ref=diagonals.at[PLANE * LANDING[hop] + to_first],
+                send_sem=diag_send, recv_sem=diag_recv, **device(0, target),
+            ).start()
+
+        if hop:
+            diagonal()
+        else:
+            pl.when(me_row != 0)(diagonal)
+            arrived[0] = sums[k, me_row]
+
+            @pl.when(me_row == 0)
+            def _():
+                diagonals[0] = sums[k, PLANE, 0:8]
+
+        for j in FAR_FIRST:
             if hop or j:
                 pltpu.make_async_remote_copy(
                     src_ref=sums.at[k, row_at[j]], dst_ref=arrived.at[PLANE * LANDING[hop] + j],
                     send_sem=send_sem, recv_sem=recv_sem, **device(row_at[j], target),
                 ).start()
-
-        def diagonal():
-            pltpu.make_async_remote_copy(
-                src_ref=sums.at[k, PLANE, pl.ds(0, 8)], dst_ref=diagonals.at[PLANE * LANDING[hop] + to_first],
-                send_sem=diag_send, recv_sem=diag_recv, **device(0, target),
-            ).start()
-
-        if hop:
-            diagonal()
-        else:
-            pl.when(me_row != 0)(diagonal)
-            arrived[0] = sums[k, me_row]
-
-            @pl.when(me_row == 0)
-            def _():
-                diagonals[0] = sums[k, PLANE, 0:8]
 
     halves = {3: pl.ds(0, PLANE // 2), 1: pl.ds(PLANE // 2, PLANE // 2 + 1)}
 
@@ -318,22 +323,11 @@
     chosen = chosen_ref[pl.ds(me_group, 1), :]
     coeffs[...] = (lax.broadcasted_iota(jnp.int32, (COLS, KEPT), 0) == chosen).astype(F32).T
 
-    others = arrived.at[pl.ds(1, SENDERS - 1)]
-    landed(others, recv_sem)
-
-    def add(i, total):
-        return total + arrived[i]
-
-    pieces[me_row] = lax.fori_loop(1, SENDERS, add, arrived[0], unroll=47)
-
     def share(j, part, send, recv):
         return pltpu.make_async_remote_copy(
             src_ref=part, dst_ref=part, send_sem=send, recv_sem=recv, **device(row_at[j], me_group)
         )
 
-    for j in range(1, PLANE):
-        share(j, pieces.at[me_row], share_send, share_recv).start()
-    fifteen = pieces.at[pl.ds(0, PLANE - 1)]
     shared_diagonal = pieces.at[PLANE, pl.ds(0, 8)]
 
     @pl.when(me_row == 0)
@@ -342,8 +336,20 @@
         pieces[PLANE, 0:8, :] = lax.fori_loop(
             1, SENDERS, lambda i, total: total + diagonals[i], diagonals[0], unroll=47
         )
-        for j in range(1, PLANE):
+        for j in FAR_FIRST[:-1]:
             share(j, shared_diagonal, share_diag_send, share_diag_recv).start()
+
+    others = arrived.at[pl.ds(1, SENDERS - 1)]
+    landed(others, recv_sem)
+
+    def add(i, total):
+        return total + arrived[i]
+
+    pieces[me_row] = lax.fori_loop(1, SENDERS, add, arrived[0], unroll=47)
+
+    for j in FAR_FIRST[:-1]:
+        share(j, pieces.at[me_row], share_send, share_recv).start()
+    fifteen = pieces.at[pl.ds(0, PLANE - 1)]
 
     @pl.when(me_row != 0)
     def _():
@@ -362,8 +368,11 @@
     step_matrix = solved(gram_f * by_row * by_col, cross_t * by_row, sub) * by_row
     moves = stacked([step_matrix, dot(gram_s, step_matrix, 1, 0)])
 
+    for i, part in enumerate(right_parts(moves, 1)):
+        moves_ref[i] = part
+
     def iterate(i, _):
-        moved = dot(coeffs[...], moves, 1, 1)
+        moved = dot(coeffs[...], None, 1, 1, [moves_ref[i] for i in range(3)])
         solution_t, weighted = moved[:, :COLS], moved[:, COLS:]
         metric = dot(solution_t, weighted, 1, 1) * (1.0 / total_rows)
         by_row, by_col = unit_scale(metric)
@@ -439,6 +448,7 @@
             pltpu.VMEM((SENDERS, *piece), F32),
             pltpu.VMEM((SENDERS, 8, COLS), F32),
             pltpu.VMEM((PLANE + 1, *piece), F32),
+            pltpu.VMEM((3, 2 * COLS, 2 * COLS), BF16),
             pltpu.VMEM((KEPT, COLS), F32),
             pltpu.VMEM((KEPT, COLS), BF16),
             dma((SYSTEMS, 2)),

time: 44.4 us -> 43.4 us (0.977)
  Pallas kernels: 44.1 us -> 43.1 us
    pallas_call x1, Pallas kernels: 40.7 us -> 39.7 us  [gathered(): pl.pallas_call(functools.partial(gather_kernel, total_rows), out_shape=[p...]
where the time goes in v6:
time: 43.4 us; the launch traced here: 43.3 us
  Pallas kernels  43.1 us (99%)
    pallas_call x1, Pallas kernels, gathered(): pl.pallas_call(functools.partial(gather_kernel, total_rows), out_shape=[p...  39.7 us
    pallas_call x1, Pallas kernels, rotated(): pl.pallas_call(rotate_kernel, out_shape=jax.ShapeDtypeStruct((SYSTEMS, DE...  3.41 us

profile of v6, /device:TPU:1, one launch (start us, length us, event | category | flops | bytes accessed | tf_op | source)
XLA Modules:
  0.0 43.3 jit_solution(15359162673055098357)
XLA Ops:
  0.0 39.7 %gather_solve.1 = (bf16[8,64,128]{2,1,0:T(8,128)(2,1)S(1)}, bf16[8,4096,256]{2,1,0:T(8,128)(2,1)S(1)}, bf16[4,4096,128]{2,1,0:T(8,128)(2,1)S(1)}) custom-call(bf16[8,4096,128]{2,1,0:T(8,128)(2,1)} %w_hbm.1, bf16[8,4096,128]{2,1,0:T(8,128)(2,1)} %q_hbm.1, s32[8,64]{1,0:T(8,128)} %chosen_hbm.1), custom_call_target="tpu_custom_call" | custom-call | tf_op jit(solution)/shard_map/gather_solve/pallas_call | solution.py:432
  39.7 3.4 %rotate.1 = bf16[8,4096,128]{2,1,0:T(8,128)(2,1)} custom-call(bf16[8,4096,256]{2,1,0:T(8,128)(2,1)S(1)} %get-tuple-element.8.wq, bf16[4,4096,128]{2,1,0:T(8,128)(2,1)S(1)} %get-tuple-element.9.turned, bf16[8,64,128]{2,1,0:T(8,128)(2,1)S(1)} %get-tuple-element.10.c_ref), custom_call_target="tpu_custom_call" | custom-call | tf_op jit(solution)/shard_map/rotate/pallas_call | solution.py:493

commit v7 on v6

--- a/solution.py
+++ b/solution.py
@@ -228,11 +228,11 @@
     fetch_chosen.start()
 
     barrier = pltpu.get_barrier_semaphore()
-    for hop in range(4):
-        pl.semaphore_signal(barrier, inc=1, **device(me_row, 2 * xs[hop] + 1 - core))
-        for j in range(PLANE if hop != 2 else 1):
+    for hop in (1, 3, 2, 0):
+        for j in FAR_FIRST if hop != 2 else (0,):
             if hop or j:
                 pl.semaphore_signal(barrier, inc=1, **device(row_at[j], 2 * xs[hop] + core))
+        pl.semaphore_signal(barrier, inc=1, **device(me_row, 2 * xs[hop] + 1 - core))
 
     across = lax.broadcasted_iota(jnp.int32, (COLS, COLS), 1)
     down = lax.broadcasted_iota(jnp.int32, (COLS, COLS), 0)

time: 43.4 us -> 43.2 us (level)
  no operation moved by 1% of the time
where the time goes in v7:
time: 43.2 us; the launch traced here: 43.1 us
  Pallas kernels  42.9 us (99%)
    pallas_call x1, Pallas kernels, gathered(): pl.pallas_call(functools.partial(gather_kernel, total_rows), out_shape=[p...  39.5 us
    pallas_call x1, Pallas kernels, rotated(): pl.pallas_call(rotate_kernel, out_shape=jax.ShapeDtypeStruct((SYSTEMS, DE...  3.41 us

profile of v7, /device:TPU:1, one launch (start us, length us, event | category | flops | bytes accessed | tf_op | source)
XLA Modules:
  0.0 43.1 jit_solution(14555248595233978290)
XLA Ops:
  0.0 39.5 %gather_solve.1 = (bf16[8,64,128]{2,1,0:T(8,128)(2,1)S(1)}, bf16[8,4096,256]{2,1,0:T(8,128)(2,1)S(1)}, bf16[4,4096,128]{2,1,0:T(8,128)(2,1)S(1)}) custom-call(bf16[8,4096,128]{2,1,0:T(8,128)(2,1)} %w_hbm.1, bf16[8,4096,128]{2,1,0:T(8,128)(2,1)} %q_hbm.1, s32[8,64]{1,0:T(8,128)} %chosen_hbm.1), custom_call_target="tpu_custom_call" | custom-call | tf_op jit(solution)/shard_map/gather_solve/pallas_call | solution.py:432
  39.5 3.4 %rotate.1 = bf16[8,4096,128]{2,1,0:T(8,128)(2,1)} custom-call(bf16[8,4096,256]{2,1,0:T(8,128)(2,1)S(1)} %get-tuple-element.8.wq, bf16[4,4096,128]{2,1,0:T(8,128)(2,1)S(1)} %get-tuple-element.9.turned, bf16[8,64,128]{2,1,0:T(8,128)(2,1)S(1)} %get-tuple-element.10.c_ref), custom_call_target="tpu_custom_call" | custom-call | tf_op jit(solution)/shard_map/rotate/pallas_call | solution.py:493
